TPU v7x, 32 devices: a whole 2x2x4 slice. The times are simulated.
32 devices in a mesh: fsdp: 8 (over y, x, core), seq: 4 (over z).
Axes of the slice: x: 2, y: 2, z: 4, core: 2. Of those that a mesh axis runs over, the one named last changes fastest.
Arguments:
- tokens: bfloat16 [8192, 2304], P('fsdp', 'seq'), may hold values from -70 to 70
- gain: float32 [2304], replicated, may hold values from 0.1 to 1.9
- w_query: bfloat16 [2304, 4096], P('fsdp', 'seq'), may hold values from -3 to 3
- w_key: bfloat16 [2304, 2048], P('fsdp', 'seq'), may hold values from -3 to 3
- w_value: bfloat16 [2304, 2048], P('fsdp', 'seq'), may hold values from -0.125 to 0.125
Outputs:
- context: bfloat16 [8192, 4096], P('fsdp', 'seq')
All inputs are finite; a program needn't handle non-finite values.
Results may differ from a plain program's by a relative error of at most 0.012.
The roundings to bfloat16 on the way count: a program that leaves them out, or rounds other values in their place, can miss the bound.
Values may be sent and summed in bfloat16 or wider, within the bound.
A program may use at most 64 MiB of HBM per device.

v0:
```python
import functools

import jax
import jax.numpy as jnp
import numpy as np
from jax import lax
from jax.experimental import pallas as pl
from jax.experimental.pallas import tpu as pltpu
from jax.sharding import PartitionSpec as P

HEAD_DIM = 128
ROWS = 256
WIRE = 128
MESH = pl.DeviceIdType.MESH


def kernel(
    n, kv, groups, chunks,
    tok_in, gain_in, cos_in, sin_in, wq_in, wk_in, wv_in, out_hbm,
    tok, w, nrm, q_s, k_s, v_s, acc, gain_ref, cos_ref, sin_ref, out_ref,
    local_sem, out_sem, t_send, t_recv, w_send, w_recv,
):
    z = lax.axis_index("seq")
    me = lax.axis_index("fsdp")
    core = lax.rem(me, 2)
    xpos = lax.rem(lax.div(me, 2), 2)
    ypos = lax.div(me, 4)
    mate = me + 1 - 2 * core
    xnbr = me + 2 - 4 * xpos
    ynbr = me + 4 - 8 * ypos
    diag = xnbr + 4 - 8 * ypos
    depth = wk_in.shape[0]
    width = wk_in.shape[1]
    cols = tok_in.shape[0]
    pieces = 2 + groups
    wire = tok_in.shape[1] // chunks

    barrier = pltpu.get_barrier_semaphore()
    for other in (mate, xnbr, ynbr):
        pl.semaphore_signal(barrier, inc=1, device_id={"fsdp": other}, device_id_type=MESH)

    @pl.when(z > 0)
    def _():
        pl.semaphore_signal(barrier, inc=1, device_id={"seq": z - 1}, device_id_type=MESH)

    @pl.when(z < n - 1)
    def _():
        pl.semaphore_signal(barrier, inc=1, device_id={"seq": z + 1}, device_id_type=MESH)

    peers = 5 - jnp.where(z == 0, 1, 0) - jnp.where(z == n - 1, 1, 0)
    pl.semaphore_wait(barrier, peers)

    def w_own(p):
        if p == 0:
            return wk_in
        if p == 1:
            return wv_in
        return wq_in.at[:, pl.ds((p - 2) * width, width)]

    def w_slot(p, f):
        return w.at[p, pl.ds(pl.multiple_of(f * depth, 16), depth), :]

    def w_copy(p, kind, lane):
        shard = (me, xnbr, ynbr, diag)[kind]
        src = w_own(p) if kind == 0 else w_slot(p, shard)
        return pltpu.make_async_remote_copy(
            src_ref=src, dst_ref=w_slot(p, shard),
            send_sem=w_send.at[lane, kind, p], recv_sem=w_recv.at[shard, p],
            device_id={"fsdp": (mate, xnbr, ynbr)[lane]}, device_id_type=MESH,
        )

    def w_wait(p, shard):
        pltpu.make_async_copy(w_slot(p, shard), w_slot(p, shard), w_recv.at[shard, p]).wait()

    def t_slot(s, c):
        return tok.at[s, :, pl.ds(c * wire if isinstance(c, int) else pl.multiple_of(c * wire, wire), wire)]

    def t_copy(block, c, side, own=False):
        src = tok_in.at[:, pl.ds(c * wire, wire)] if own else t_slot(block, c)
        return pltpu.make_async_remote_copy(
            src_ref=src, dst_ref=t_slot(block, c),
            send_sem=t_send.at[side, block, c], recv_sem=t_recv.at[block, c],
            device_id={"seq": z + 1 - 2 * side}, device_id_type=MESH,
        )

    def t_wait(block, c):
        pltpu.make_async_copy(t_slot(block, c), t_slot(block, c), t_recv.at[block, c]).wait()

    def own_tokens(c, do):
        @pl.when(z < n - 1)
        def _():
            do(t_copy(z, c, 0, True))

        @pl.when(z > 0)
        def _():
            do(t_copy(z, c, 1, True))

    def own_weights(do):
        for p in range(pieces):
            for lane in (1, 2, 0):
                do(w_copy(p, 0, lane))

    def start(copy):
        copy.start()

    for c in range(2):
        own_tokens(c, start)
    own_weights(start)
    local = [pltpu.make_async_copy(tok_in, tok.at[z], local_sem.at[0])]
    for p in range(pieces):
        local.append(pltpu.make_async_copy(w_own(p), w_slot(p, me), local_sem.at[p + 1]))
    local.append(pltpu.make_async_copy(gain_in, gain_ref.at[0], local_sem.at[pieces + 1]))
    local.append(pltpu.make_async_copy(cos_in, cos_ref, local_sem.at[pieces + 2]))
    local.append(pltpu.make_async_copy(sin_in, sin_ref, local_sem.at[pieces + 3]))
    for copy in local:
        copy.start()
    v_s[:, :, HEAD_DIM:] = jnp.ones((kv, v_s.shape[1], HEAD_DIM), jnp.bfloat16)

    def relay(dist, c):
        @pl.when((z >= dist) & (z < n - 1))
        def _():
            t_wait(z - dist, c)
            t_copy(z - dist, c, 0).start()

        @pl.when((z + dist < n) & (z > 0))
        def _():
            t_wait(z + dist, c)
            t_copy(z + dist, c, 1).start()

    def settle(dist, c):
        @pl.when((z >= dist) & (z == n - 1))
        def _():
            t_wait(z - dist, c)

        @pl.when((z + dist < n) & (z == 0))
        def _():
            t_wait(z + dist, c)

    def token_round(k):
        for dist in range(n - 2, 0, -1):
            c = k - dist + 1
            if 0 <= c < chunks:
                relay(dist, c)
        if k + 2 < chunks:
            own_tokens(k + 2, start)

    rounds = chunks + n - 3
    early = min(n + 2, rounds)
    for step in range(max(early, pieces)):
        if step < early:
            token_round(step)
        if step < pieces:
            w_wait(step, xnbr)
            w_copy(step, 1, 0).start()

            @pl.when(core == 1)
            def _():
                w_copy(step, 1, 2).start()

            w_wait(step, ynbr)
            w_copy(step, 2, 0).start()

            @pl.when(core == 0)
            def _():
                w_copy(step, 2, 1).start()

    for p in range(pieces):
        w_wait(p, diag)
        w_copy(p, 3, 0).start()
    for p in range(pieces):
        for shard in (mate, xnbr + 1 - 2 * core, ynbr + 1 - 2 * core, diag + 1 - 2 * core):
            w_wait(p, shard)
    for copy in local:
        copy.wait()

    scale = 1.0 / (12.0 * 50.0)

    R = wire

    def out_copy(first, part):
        rows = pl.ds(first, R)
        return pltpu.make_async_copy(out_ref.at[rows, :], out_hbm.at[rows, :], out_sem.at[part])

    def chunk(first, low, last, base_count, part):
        rows = pl.ds(first, R)
        for dist in range(1, n):
            settle(dist, part)
        raw = jnp.concatenate([tok[s, :, rows] for s in range(n)], axis=0).T
        floats = raw.astype(jnp.float32)
        total = jnp.sum(floats * floats, axis=-1, keepdims=True)
        inv = lax.rsqrt(total / (n * cols) + 1e-06)
        nrm[:R, :] = (floats * inv * gain_ref[...]).astype(jnp.bfloat16)
        normed = nrm[:R, :]
        cosine = cos_ref[rows, :]
        sine = sin_ref[rows, :]

        def rotate(x):
            return (x * cosine + pltpu.roll(x, HEAD_DIM // 2, 1) * sine).astype(jnp.bfloat16)

        raw = jnp.dot(normed, w[0], preferred_element_type=jnp.float32)
        for h in range(kv):
            k_s[h, rows, :] = rotate(raw[:, h * HEAD_DIM : (h + 1) * HEAD_DIM])
        raw = jnp.dot(normed, w[1], preferred_element_type=jnp.float32)
        for h in range(kv):
            v_s[h, rows, :HEAD_DIM] = raw[:, h * HEAD_DIM : (h + 1) * HEAD_DIM].astype(jnp.bfloat16)
        for g in range(groups):
            raw = jnp.dot(normed, w[2 + g], preferred_element_type=jnp.float32)
            for i in range(kv):
                head = g * kv + i
                at = (head % groups) * R
                q_s[head // groups, at : at + R, :] = rotate(
                    raw[:, i * HEAD_DIM : (i + 1) * HEAD_DIM]
                )

        def block(h, keys, mask):
            s = lax.dot_general(
                q_s[h, : groups * R, :], k_s[h, keys, :], (((1,), (1,)), ((), ())),
                preferred_element_type=jnp.float32,
            )
            e = jnp.exp(jnp.tanh(s * scale) * 50.0)
            if mask is not None:
                e = jnp.where(mask, e, 0.0)
            return jnp.dot(
                e.astype(jnp.bfloat16), v_s[h, keys, :], preferred_element_type=jnp.float32
            )

        row_id = lax.rem(lax.broadcasted_iota(jnp.int32, (groups * R, last), 0), R)
        mask = lax.broadcasted_iota(jnp.int32, (groups * R, last), 1) <= row_id + (last - R)
        top = pl.ds(low, last)
        for h in range(kv):
            acc[h, : groups * R, :] = block(h, top, mask)

        def inner(j, carry):
            keys = pl.ds(pl.multiple_of(j * ROWS, ROWS), ROWS)
            for h in range(kv):
                acc[h, : groups * R, :] += block(h, keys, None)
            return carry

        lax.fori_loop(0, base_count, inner, 0)
        for h in range(kv):
            for g in range(groups):
                sums = acc[h, g * R : (g + 1) * R, :]
                head = h * groups + g
                out_ref[rows, head * HEAD_DIM : (head + 1) * HEAD_DIM] = (
                    sums[:, :HEAD_DIM] / sums[:, HEAD_DIM:]
                ).astype(jnp.bfloat16)
        out_copy(first, part).start()

    def body(c, carry):
        @pl.when(c == 0)
        def _():
            if early < rounds:
                token_round(early)

        @pl.when(c == 1)
        def _():
            for k in range(early + 1, rounds):
                token_round(k)

        low = pl.multiple_of(c * ROWS, ROWS)
        for i in range(ROWS // R):
            first = pl.multiple_of(c * ROWS + i * R, R)
            chunk(first, low, (i + 1) * R, c, c * (ROWS // R) + i)
        return carry

    lax.fori_loop(0, chunks * wire // ROWS, body, 0)
    for part in range(chunks):
        out_copy(part * R, part).wait()

    own_weights(lambda copy: copy.wait_send())
    for c in range(chunks):
        own_tokens(c, lambda copy: copy.wait_send())
        for dist in range(1, n - 1):
            @pl.when((z >= dist) & (z < n - 1))
            def _():
                t_copy(z - dist, c, 0).wait_send()

            @pl.when((z + dist < n) & (z > 0))
            def _():
                t_copy(z + dist, c, 1).wait_send()

    for p in range(pieces):
        for kind in (1, 2, 3):
            w_copy(p, kind, 0).wait_send()

        @pl.when(core == 1)
        def _():
            w_copy(p, 1, 2).wait_send()

        @pl.when(core == 0)
        def _():
            w_copy(p, 2, 1).wait_send()


def fused(n, fsdp, tokens, gain, w_query, w_key, w_value):
    length, cols = tokens.shape
    depth, width = w_key.shape
    kv = width // HEAD_DIM
    groups = w_query.shape[1] // width
    chunks = length // WIRE
    half = HEAD_DIM // 2
    freqs = 10000.0 ** (-2.0 * np.arange(half) / HEAD_DIM)
    angle = np.arange(length)[:, None] * freqs[None, :]
    cosine = np.concatenate([np.cos(angle)] * 2, axis=1).astype(np.float32)
    sine = np.concatenate([-np.sin(angle), np.sin(angle)], axis=1).astype(np.float32)
    hbm = pl.BlockSpec(memory_space=pl.ANY)
    pieces = 2 + groups
    flops = 2 * length * fsdp * depth * width * pieces
    return pl.pallas_call(
        functools.partial(kernel, n, kv, groups, chunks),
        out_shape=jax.ShapeDtypeStruct((length, w_query.shape[1]), jnp.bfloat16),
        in_specs=[hbm] * 7,
        out_specs=hbm,
        scratch_shapes=[
            pltpu.VMEM((n, cols, length), jnp.bfloat16),
            pltpu.VMEM((pieces, fsdp * depth, width), jnp.bfloat16),
            pltpu.VMEM((WIRE, n * cols), jnp.bfloat16),
            pltpu.VMEM((kv, groups * WIRE, HEAD_DIM), jnp.bfloat16),
            pltpu.VMEM((kv, length, HEAD_DIM), jnp.bfloat16),
            pltpu.VMEM((kv, length, 2 * HEAD_DIM), jnp.bfloat16),
            pltpu.VMEM((kv, groups * WIRE, 2 * HEAD_DIM), jnp.float32),
            pltpu.VMEM((1, n * cols), jnp.float32),
            pltpu.VMEM((length, HEAD_DIM), jnp.float32),
            pltpu.VMEM((length, HEAD_DIM), jnp.float32),
            pltpu.VMEM((length, w_query.shape[1]), jnp.bfloat16),
            pltpu.SemaphoreType.DMA((4 + pieces,)),
            pltpu.SemaphoreType.DMA((chunks,)),
            pltpu.SemaphoreType.DMA((2, n, chunks)),
            pltpu.SemaphoreType.DMA((n, chunks)),
            pltpu.SemaphoreType.DMA((3, 4, pieces)),
            pltpu.SemaphoreType.DMA((fsdp, pieces)),
        ],
        compiler_params=pltpu.CompilerParams(
            collective_id=0, has_side_effects=True, vmem_limit_bytes=60 * 1024 * 1024
        ),
        cost_estimate=pl.CostEstimate(flops=flops, bytes_accessed=2 * length * cols, transcendentals=0),
    )(tokens.T, gain, jnp.asarray(cosine), jnp.asarray(sine), w_query, w_key, w_value)


def rotate(values, positions):
    half = values.shape[-1] // 2
    index = jnp.arange(half, dtype=jnp.float32)
    freqs = jnp.power(jnp.float32(10000.0), -2.0 * index / values.shape[-1])
    angle = positions[:, None] * freqs[None, :]
    cosine = jnp.cos(angle)[:, None, :]
    sine = jnp.sin(angle)[:, None, :]
    first = values[..., :half]
    second = values[..., half:]
    return jnp.concatenate(
        [first * cosine - second * sine, second * cosine + first * sine], axis=-1
    )


def local(tokens, gain, w_query, w_key, w_value):
    features = gain.shape[0]
    floats = tokens.astype(jnp.float32)
    square_sum = lax.psum(jnp.sum(floats * floats, axis=-1), "seq")
    inv_rms = lax.rsqrt(square_sum / features + 1e-06)[:, None]
    own_cols = tokens.shape[1]
    gain_part = lax.dynamic_slice_in_dim(gain, lax.axis_index("seq") * own_cols, own_cols, 0)
    own_normed = (floats * inv_rms * gain_part[None, :]).astype(jnp.bfloat16)
    normed = lax.all_gather(own_normed, "seq", axis=1, tiled=True)
    length = normed.shape[0]

    def add_one(piece):
        return jnp.dot(normed, piece, preferred_element_type=jnp.float32)

    query_raw = add_one(lax.all_gather(w_query, "fsdp", axis=0, tiled=True))
    key_raw = add_one(lax.all_gather(w_key, "fsdp", axis=0, tiled=True))
    value_raw = add_one(lax.all_gather(w_value, "fsdp", axis=0, tiled=True))
    local_heads = w_query.shape[1] // HEAD_DIM
    local_kv = w_key.shape[1] // HEAD_DIM
    groups = local_heads // local_kv
    positions = jnp.arange(length, dtype=jnp.float32)
    values = value_raw.astype(jnp.bfloat16).reshape(length, local_kv, HEAD_DIM)
    query = rotate(query_raw.reshape(length, local_heads, HEAD_DIM), positions).astype(jnp.bfloat16)
    query = query.reshape(length, local_kv, groups, HEAD_DIM)
    keys = rotate(key_raw.reshape(length, local_kv, HEAD_DIM), positions).astype(jnp.bfloat16)
    scale = 1.0 / jnp.sqrt(jnp.float32(144.0))
    block_rows = 512
    outputs = []
    for first_row in range(0, length, block_rows):
        extent = first_row + block_rows
        query_block = query[first_row:extent]
        scores = (
            jnp.einsum(
                "lgqd,mgd->gqlm", query_block, keys[:extent], preferred_element_type=jnp.float32
            )
            * scale
        )
        capped = 50.0 * jnp.tanh(scores / 50.0)
        causal = jnp.arange(extent)[None, :] <= (first_row + jnp.arange(block_rows))[:, None]
        exponent = jnp.where(causal[None, None], jnp.exp(capped), 0.0)
        weights = (exponent / jnp.sum(exponent, axis=-1, keepdims=True)).astype(jnp.bfloat16)
        context = jnp.einsum(
            "gqlm,mgd->lgqd", weights, values[:extent], preferred_element_type=jnp.float32
        )
        outputs.append(context.reshape(block_rows, local_heads * HEAD_DIM).astype(jnp.bfloat16))
    return jnp.concatenate(outputs, axis=0)


def solution(mesh):
    n, fsdp = mesh.shape["seq"], mesh.shape["fsdp"]
    in_specs = (P("fsdp", "seq"), P(), P("fsdp", "seq"), P("fsdp", "seq"), P("fsdp", "seq"))
    out_specs = P("fsdp", "seq")

    def step(tokens, gain, w_query, w_key, w_value):
        fits = (
            fsdp == 8
            and n == 4
            and tokens.shape[1] % 16 == 0
            and tokens.shape[0] % ROWS == 0
            and tokens.shape[0] >= 3 * ROWS
            and w_key.shape[0] % 16 == 0
            and w_query.shape[1] % w_key.shape[1] == 0
        )
        if fits:
            return fused(n, fsdp, tokens, gain, w_query, w_key, w_value)
        return local(tokens, gain, w_query, w_key, w_value)

    return jax.shard_map(step, mesh=mesh, in_specs=in_specs, out_specs=out_specs, check_vma=False)
```

profile of v0, /device:TPU:1, one launch (start us, length us, event | category | flops | bytes accessed | tf_op | source)
XLA Modules:
  0.0 89.2 jit_solution(568341611270224250)
XLA Ops:
  0.0 86.1 %shard_map.73 = bf16[1024,1024]{1,0:T(8,128)(2,1)} custom-call(bf16[576,1024]{1,0:T(8,128)(2,1)} %bitcast.1, f32[2304]{0:T(1024)} %gain_in.1, f32[1024,128]{1,0:T(8,128)} %constant.4.clone.cos_in, f32[1024,128]{1,0:T(8,128)} %constant.5.clone.sin_in, bf16[288,1024]{1,0:T(8,128)(2,1)} %wq_in.1, bf16[288,512]{1,0:T(8,128)(2,1)} %wk_in.1, bf16[288,512]{1,0:T(8,128)(2,1)} %wv_in.1), custom_call_target="tpu_custom_call" | custom-call | flops 9663676416 | bytes 1179648 | tf_op jit(solution)/shard_map/pallas_call | solution.py:309
  86.1 3.1 %copy.9 = bf16[1024,1024]{1,0:T(8,128)(2,1)} copy(bf16[1024,1024]{1,0:T(8,128)(2,1)} %shard_map.73) | data formatting | bytes 4194304
where the time goes:
time: 90.8 us; the launch traced here: 89.2 us
  Pallas kernels  86.1 us (95%)
  local copies, waits for them, and re-layouts  3.08 us (3%)
    pallas_call x1, Pallas kernels, fused(): pl.pallas_call(functools.partial(kernel, n, kv, groups, chunks), out_shap...  86.1 us
    unnamed x1, local copies, waits for them, and re-layouts  3.08 us

commit v1 on v0

--- a/solution.py
+++ b/solution.py
@@ -1,4 +1,5 @@
 import functools
+import math
 
 import jax
 import jax.numpy as jnp
@@ -17,8 +18,8 @@
 def kernel(
     n, kv, groups, chunks,
     tok_in, gain_in, cos_in, sin_in, wq_in, wk_in, wv_in, out_hbm,
-    tok, w, nrm, q_s, k_s, v_s, acc, gain_ref, cos_ref, sin_ref, out_ref,
-    local_sem, out_sem, t_send, t_recv, w_send, w_recv,
+    tok, w, nrm, q_s, k_s, v_s, acc, gain_ref, cos_ref, sin_ref, part_ref, ss,
+    tok_sem, local_sem, t_send, t_recv, w_send, w_recv, s_send, s_recv,
 ):
     z = lax.axis_index("seq")
     me = lax.axis_index("fsdp")
@@ -35,6 +36,17 @@
     pieces = 2 + groups
     wire = tok_in.shape[1] // chunks
 
+    def own_slot(first, size):
+        rows = pl.ds(pl.multiple_of(z * cols, 16), cols)
+        return tok.at[rows, pl.ds(first, size)]
+
+    def load(first, size, i):
+        return pltpu.make_async_copy(tok_in.at[:, pl.ds(first, size)], own_slot(first, size), tok_sem.at[i])
+
+    loads = [load(0, wire, 0), load(wire, wire, 1), load(2 * wire, tok_in.shape[1] - 2 * wire, 2)]
+    for copy in loads:
+        copy.start()
+
     barrier = pltpu.get_barrier_semaphore()
     for other in (mate, xnbr, ynbr):
         pl.semaphore_signal(barrier, inc=1, device_id={"fsdp": other}, device_id_type=MESH)
@@ -73,12 +85,12 @@
         pltpu.make_async_copy(w_slot(p, shard), w_slot(p, shard), w_recv.at[shard, p]).wait()
 
     def t_slot(s, c):
-        return tok.at[s, :, pl.ds(c * wire if isinstance(c, int) else pl.multiple_of(c * wire, wire), wire)]
-
-    def t_copy(block, c, side, own=False):
-        src = tok_in.at[:, pl.ds(c * wire, wire)] if own else t_slot(block, c)
+        first = c * wire if isinstance(c, int) else pl.multiple_of(c * wire, wire)
+        return tok.at[pl.ds(pl.multiple_of(s * cols, 16), cols), pl.ds(first, wire)]
+
+    def t_copy(block, c, side):
         return pltpu.make_async_remote_copy(
-            src_ref=src, dst_ref=t_slot(block, c),
+            src_ref=t_slot(block, c), dst_ref=t_slot(block, c),
             send_sem=t_send.at[side, block, c], recv_sem=t_recv.at[block, c],
             device_id={"seq": z + 1 - 2 * side}, device_id_type=MESH,
         )
@@ -89,11 +101,11 @@
     def own_tokens(c, do):
         @pl.when(z < n - 1)
         def _():
-            do(t_copy(z, c, 0, True))
+            do(t_copy(z, c, 0))
 
         @pl.when(z > 0)
         def _():
-            do(t_copy(z, c, 1, True))
+            do(t_copy(z, c, 1))
 
     def own_weights(do):
         for p in range(pieces):
@@ -103,19 +115,47 @@
     def start(copy):
         copy.start()
 
-    for c in range(2):
-        own_tokens(c, start)
+    def s_copy(block, side):
+        return pltpu.make_async_remote_copy(
+            src_ref=ss.at[block], dst_ref=ss.at[block],
+            send_sem=s_send.at[side, block], recv_sem=s_recv.at[block],
+            device_id={"seq": z + 1 - 2 * side}, device_id_type=MESH,
+        )
+
+    def s_wait(block):
+        pltpu.make_async_copy(ss.at[block], ss.at[block], s_recv.at[block]).wait()
+
+    def own_sums(do):
+        @pl.when(z < n - 1)
+        def _():
+            do(s_copy(z, 0))
+
+        @pl.when(z > 0)
+        def _():
+            do(s_copy(z, 1))
+
+    def first_tokens():
+        for c in range(2):
+            loads[c].wait()
+            own_tokens(c, start)
+
+    first_tokens()
+
     own_weights(start)
-    local = [pltpu.make_async_copy(tok_in, tok.at[z], local_sem.at[0])]
+    local = []
     for p in range(pieces):
-        local.append(pltpu.make_async_copy(w_own(p), w_slot(p, me), local_sem.at[p + 1]))
-    local.append(pltpu.make_async_copy(gain_in, gain_ref.at[0], local_sem.at[pieces + 1]))
-    local.append(pltpu.make_async_copy(cos_in, cos_ref, local_sem.at[pieces + 2]))
-    local.append(pltpu.make_async_copy(sin_in, sin_ref, local_sem.at[pieces + 3]))
+        local.append(pltpu.make_async_copy(w_own(p), w_slot(p, me), local_sem.at[p]))
+    local.append(pltpu.make_async_copy(gain_in, gain_ref.at[0], local_sem.at[pieces]))
+    local.append(pltpu.make_async_copy(cos_in, cos_ref, local_sem.at[pieces + 1]))
+    local.append(pltpu.make_async_copy(sin_in, sin_ref, local_sem.at[pieces + 2]))
     for copy in local:
         copy.start()
     v_s[:, :, HEAD_DIM:] = jnp.ones((kv, v_s.shape[1], HEAD_DIM), jnp.bfloat16)
 
+    loads[2].wait()
+    last = t_slot(z, chunks - 1)[...].astype(jnp.float32)
+    ss[z] = jnp.sum(last * last, axis=0, keepdims=True)
+
     def relay(dist, c):
         @pl.when((z >= dist) & (z < n - 1))
         def _():
@@ -126,6 +166,17 @@
         def _():
             t_wait(z + dist, c)
             t_copy(z + dist, c, 1).start()
+
+    def relay_sums(dist):
+        @pl.when((z >= dist) & (z < n - 1))
+        def _():
+            s_wait(z - dist)
+            s_copy(z - dist, 0).start()
+
+        @pl.when((z + dist < n) & (z > 0))
+        def _():
+            s_wait(z + dist)
+            s_copy(z + dist, 1).start()
 
     def settle(dist, c):
         @pl.when((z >= dist) & (z == n - 1))
@@ -149,6 +200,10 @@
     for step in range(max(early, pieces)):
         if step < early:
             token_round(step)
+        if step == 1:
+            own_sums(start)
+        if 2 <= step < n:
+            relay_sums(step - 1)
         if step < pieces:
             w_wait(step, xnbr)
             w_copy(step, 1, 0).start()
@@ -174,28 +229,99 @@
         copy.wait()
 
     scale = 1.0 / (12.0 * 50.0)
+    peak = 50.0 * math.log2(math.e)
 
     R = wire
 
-    def out_copy(first, part):
+    def rotate_at(rows):
+        cosine = cos_ref[rows, :]
+        sine = sin_ref[rows, :]
+        return lambda x: (x * cosine + pltpu.roll(x, HEAD_DIM // 2, 1) * sine).astype(jnp.bfloat16)
+
+    def tail():
+        length = chunks * wire
+        first = length - R
         rows = pl.ds(first, R)
-        return pltpu.make_async_copy(out_ref.at[rows, :], out_hbm.at[rows, :], out_sem.at[part])
+        near = (n - 1) * cols
+        left = z == 0
+        near_at = pl.ds(pl.multiple_of(jnp.where(left, 0, cols), 16), near)
+        far_at = pl.ds(pl.multiple_of(jnp.where(left, near, 0), 16), cols)
+        for dist in range(1, n):
+            @pl.when(left)
+            def _():
+                s_wait(z + dist)
+
+            @pl.when(z == n - 1)
+            def _():
+                s_wait(z - dist)
+
+        for dist in range(1, n - 1):
+            settle(dist, chunks - 1)
+        total = ss[0]
+        for s in range(1, n):
+            total += ss[s]
+        inv = lax.rsqrt(total / (n * cols) + 1e-06)
+        inv = jnp.broadcast_to(inv, (R, R)).T[:, :1]
+        gain = gain_ref[...]
+        near_gain = jnp.where(left, gain[:, :near], gain[:, cols:])
+        far_gain = jnp.where(left, gain[:, near:], gain[:, :cols])
+        floats = tok[near_at, rows].T.astype(jnp.float32)
+        normed = (floats * inv * near_gain).astype(jnp.bfloat16)
+        for p in range(pieces):
+            part_ref[p] = jnp.dot(normed, w[p, near_at, :], preferred_element_type=jnp.float32)
+        settle(n - 1, chunks - 1)
+        floats = tok[far_at, rows].T.astype(jnp.float32)
+        normed = (floats * inv * far_gain).astype(jnp.bfloat16)
+        turn = rotate_at(rows)
+
+        def project(p):
+            return part_ref[p] + jnp.dot(normed, w[p, far_at, :], preferred_element_type=jnp.float32)
+
+        raw = project(0)
+        for h in range(kv):
+            k_s[h, rows, :] = turn(raw[:, h * HEAD_DIM : (h + 1) * HEAD_DIM])
+        raw = project(1)
+        for h in range(kv):
+            v_s[h, rows, :HEAD_DIM] = raw[:, h * HEAD_DIM : (h + 1) * HEAD_DIM].astype(jnp.bfloat16)
+        for g in range(groups):
+            raw = project(2 + g)
+            for i in range(kv):
+                head = g * kv + i
+                at = (head % groups) * R
+                q_s[head // groups, at : at + R, :] = turn(raw[:, i * HEAD_DIM : (i + 1) * HEAD_DIM])
+        row_id = lax.rem(lax.broadcasted_iota(jnp.int32, (groups * R, ROWS), 0), R)
+        mask = lax.broadcasted_iota(jnp.int32, (groups * R, ROWS), 1) <= row_id + (ROWS - R)
+        for h in range(kv):
+            sums = None
+            for low in range(0, length, ROWS):
+                keys = pl.ds(low, ROWS)
+                s = lax.dot_general(
+                    q_s[h, : groups * R, :], k_s[h, keys, :], (((1,), (1,)), ((), ())),
+                    preferred_element_type=jnp.float32,
+                )
+                e = jnp.exp2(jnp.tanh(s * scale) * peak)
+                if low + ROWS == length:
+                    e = jnp.where(mask, e, 0.0)
+                e = jnp.dot(e.astype(jnp.bfloat16), v_s[h, keys, :], preferred_element_type=jnp.float32)
+                sums = e if sums is None else sums + e
+            for g in range(groups):
+                head = h * groups + g
+                part = sums[g * R : (g + 1) * R, :]
+                out_hbm[rows, head * HEAD_DIM : (head + 1) * HEAD_DIM] = (
+                    part[:, :HEAD_DIM] / part[:, HEAD_DIM:]
+                ).astype(jnp.bfloat16)
 
     def chunk(first, low, last, base_count, part):
         rows = pl.ds(first, R)
         for dist in range(1, n):
             settle(dist, part)
-        raw = jnp.concatenate([tok[s, :, rows] for s in range(n)], axis=0).T
+        raw = tok[:, rows].T
         floats = raw.astype(jnp.float32)
         total = jnp.sum(floats * floats, axis=-1, keepdims=True)
         inv = lax.rsqrt(total / (n * cols) + 1e-06)
         nrm[:R, :] = (floats * inv * gain_ref[...]).astype(jnp.bfloat16)
         normed = nrm[:R, :]
-        cosine = cos_ref[rows, :]
-        sine = sin_ref[rows, :]
-
-        def rotate(x):
-            return (x * cosine + pltpu.roll(x, HEAD_DIM // 2, 1) * sine).astype(jnp.bfloat16)
+        rotate = rotate_at(rows)
 
         raw = jnp.dot(normed, w[0], preferred_element_type=jnp.float32)
         for h in range(kv):
@@ -217,7 +343,7 @@
                 q_s[h, : groups * R, :], k_s[h, keys, :], (((1,), (1,)), ((), ())),
                 preferred_element_type=jnp.float32,
             )
-            e = jnp.exp(jnp.tanh(s * scale) * 50.0)
+            e = jnp.exp2(jnp.tanh(s * scale) * peak)
             if mask is not None:
                 e = jnp.where(mask, e, 0.0)
             return jnp.dot(
@@ -241,10 +367,9 @@
             for g in range(groups):
                 sums = acc[h, g * R : (g + 1) * R, :]
                 head = h * groups + g
-                out_ref[rows, head * HEAD_DIM : (head + 1) * HEAD_DIM] = (
+                out_hbm[rows, head * HEAD_DIM : (head + 1) * HEAD_DIM] = (
                     sums[:, :HEAD_DIM] / sums[:, HEAD_DIM:]
                 ).astype(jnp.bfloat16)
-        out_copy(first, part).start()
 
     def body(c, carry):
         @pl.when(c == 0)
@@ -258,14 +383,34 @@
                 token_round(k)
 
         low = pl.multiple_of(c * ROWS, ROWS)
-        for i in range(ROWS // R):
+        per = ROWS // R
+        for i in range(per):
             first = pl.multiple_of(c * ROWS + i * R, R)
-            chunk(first, low, (i + 1) * R, c, c * (ROWS // R) + i)
+            part = c * per + i
+            if i < per - 1:
+                chunk(first, low, (i + 1) * R, c, part)
+            else:
+                @pl.when((part < chunks - 1) | ((z > 0) & (z < n - 1)))
+                def _():
+                    chunk(first, low, (i + 1) * R, c, part)
         return carry
 
     lax.fori_loop(0, chunks * wire // ROWS, body, 0)
-    for part in range(chunks):
-        out_copy(part * R, part).wait()
+
+    @pl.when((z == 0) | (z == n - 1))
+    def _():
+        tail()
+
+
+    own_sums(lambda copy: copy.wait_send())
+    for dist in range(1, n - 1):
+        @pl.when((z >= dist) & (z < n - 1))
+        def _():
+            s_copy(z - dist, 0).wait_send()
+
+        @pl.when((z + dist < n) & (z > 0))
+        def _():
+            s_copy(z + dist, 1).wait_send()
 
     own_weights(lambda copy: copy.wait_send())
     for c in range(chunks):
@@ -308,11 +453,11 @@
     flops = 2 * length * fsdp * depth * width * pieces
     return pl.pallas_call(
         functools.partial(kernel, n, kv, groups, chunks),
-        out_shape=jax.ShapeDtypeStruct((length, w_query.shape[1]), jnp.bfloat16),
+        out_shape=pltpu.VMEM((length, w_query.shape[1]), jnp.bfloat16),
         in_specs=[hbm] * 7,
-        out_specs=hbm,
+        out_specs=pl.BlockSpec(memory_space=pltpu.VMEM),
         scratch_shapes=[
-            pltpu.VMEM((n, cols, length), jnp.bfloat16),
+            pltpu.VMEM((n * cols, length), jnp.bfloat16),
             pltpu.VMEM((pieces, fsdp * depth, width), jnp.bfloat16),
             pltpu.VMEM((WIRE, n * cols), jnp.bfloat16),
             pltpu.VMEM((kv, groups * WIRE, HEAD_DIM), jnp.bfloat16),
@@ -322,13 +467,16 @@
             pltpu.VMEM((1, n * cols), jnp.float32),
             pltpu.VMEM((length, HEAD_DIM), jnp.float32),
             pltpu.VMEM((length, HEAD_DIM), jnp.float32),
-            pltpu.VMEM((length, w_query.shape[1]), jnp.bfloat16),
-            pltpu.SemaphoreType.DMA((4 + pieces,)),
-            pltpu.SemaphoreType.DMA((chunks,)),
+            pltpu.VMEM((pieces, WIRE, width), jnp.float32),
+            pltpu.VMEM((n, 1, WIRE), jnp.float32),
+            pltpu.SemaphoreType.DMA((3,)),
+            pltpu.SemaphoreType.DMA((3 + pieces,)),
             pltpu.SemaphoreType.DMA((2, n, chunks)),
             pltpu.SemaphoreType.DMA((n, chunks)),
             pltpu.SemaphoreType.DMA((3, 4, pieces)),
             pltpu.SemaphoreType.DMA((fsdp, pieces)),
+            pltpu.SemaphoreType.DMA((2, n)),
+            pltpu.SemaphoreType.DMA((n,)),
         ],
         compiler_params=pltpu.CompilerParams(
             collective_id=0, has_side_effects=True, vmem_limit_bytes=60 * 1024 * 1024

time: 90.8 us -> 86.3 us (0.950)
  Pallas kernels: 86.1 us -> 83.3 us
  local copies, waits for them, and re-layouts: 3.08 us -> 1.32 us
    pallas_call x1, Pallas kernels: 86.1 us -> 83.3 us  [fused(): pl.pallas_call(functools.partial(kernel, n, kv, groups, chunks), out_shap...]
    unnamed x1, local copies, waits for them, and re-layouts: 3.08 us -> 1.32 us
where the time goes in v1:
time: 86.3 us; the launch traced here: 84.6 us
  Pallas kernels  83.3 us (97%)
  local copies, waits for them, and re-layouts  1.32 us (2%)
    pallas_call x1, Pallas kernels, fused(): pl.pallas_call(functools.partial(kernel, n, kv, groups, chunks), out_shap...  83.3 us

profile of v1, /device:TPU:1, one launch (start us, length us, event | category | flops | bytes accessed | tf_op | source)
XLA Modules:
  0.0 84.6 jit_solution(11191901662077648292)
XLA Ops:
  0.0 83.3 %shard_map.73 = bf16[1024,1024]{1,0:T(8,128)(2,1)S(1)} custom-call(bf16[576,1024]{1,0:T(8,128)(2,1)} %bitcast.1, f32[2304]{0:T(1024)} %gain_in.1, f32[1024,128]{1,0:T(8,128)} %constant.4.clone.cos_in, f32[1024,128]{1,0:T(8,128)} %constant.5.clone.sin_in, bf16[288,1024]{1,0:T(8,128)(2,1)} %wq_in.1, bf16[288,512]{1,0:T(8,128)(2,1)} %wk_in.1, ...), custom_call_target="tpu_custom_call" | custom-call | flops 9663676416 | bytes 1179648 | tf_op jit(solution)/shard_map/pallas_call | solution.py:454
  83.3 1.3 %copy.9 = bf16[1024,1024]{1,0:T(8,128)(2,1)} copy(bf16[1024,1024]{1,0:T(8,128)(2,1)S(1)} %shard_map.73) | data formatting | bytes 4194304

commit v2 on v1

--- a/solution.py
+++ b/solution.py
@@ -12,6 +12,7 @@
 HEAD_DIM = 128
 ROWS = 256
 WIRE = 128
+LATE = 256
 MESH = pl.DeviceIdType.MESH
 
 
@@ -72,40 +73,69 @@
     def w_slot(p, f):
         return w.at[p, pl.ds(pl.multiple_of(f * depth, 16), depth), :]
 
+    def w_mark(p, kind, lane):
+        if lane == 0:
+            return w_recv.at[3 * pieces]
+        return w_recv.at[(lane - 1 if kind == 0 else 2) * pieces + p]
+
     def w_copy(p, kind, lane):
         shard = (me, xnbr, ynbr, diag)[kind]
         src = w_own(p) if kind == 0 else w_slot(p, shard)
         return pltpu.make_async_remote_copy(
             src_ref=src, dst_ref=w_slot(p, shard),
-            send_sem=w_send.at[lane, kind, p], recv_sem=w_recv.at[shard, p],
+            send_sem=w_send.at[0], recv_sem=w_mark(p, kind, lane),
             device_id={"fsdp": (mate, xnbr, ynbr)[lane]}, device_id_type=MESH,
         )
 
-    def w_wait(p, shard):
-        pltpu.make_async_copy(w_slot(p, shard), w_slot(p, shard), w_recv.at[shard, p]).wait()
+    def w_wait(p, i):
+        slot = w_slot(p, (xnbr, ynbr, diag)[i])
+        pltpu.make_async_copy(slot, slot, w_recv.at[i * pieces + p]).wait()
+
+    def w_bulk(count, sem):
+        slots = w.at[:, pl.ds(0, count * depth), :]
+        pltpu.make_async_copy(slots, slots, sem).wait()
 
     def t_slot(s, c):
         first = c * wire if isinstance(c, int) else pl.multiple_of(c * wire, wire)
         return tok.at[pl.ds(pl.multiple_of(s * cols, 16), cols), pl.ds(first, wire)]
 
-    def t_copy(block, c, side):
-        return pltpu.make_async_remote_copy(
-            src_ref=t_slot(block, c), dst_ref=t_slot(block, c),
-            send_sem=t_send.at[side, block, c], recv_sem=t_recv.at[block, c],
-            device_id={"seq": z + 1 - 2 * side}, device_id_type=MESH,
-        )
-
-    def t_wait(block, c):
-        pltpu.make_async_copy(t_slot(block, c), t_slot(block, c), t_recv.at[block, c]).wait()
+    def t_pieces(block, c, side):
+        if not isinstance(c, int) or c < chunks - 1:
+            return [(t_slot(block, c), c)]
+        early_at, late_at = (LATE, 0) if side == 0 else (0, cols - LATE)
+        lanes = pl.ds(c * wire, wire)
+        pieces_of = []
+        for at, size, i in ((early_at, cols - LATE, c), (late_at, LATE, chunks)):
+            rows = pl.ds(pl.multiple_of(block * cols + at, 16), size)
+            pieces_of.append((tok.at[rows, lanes], i))
+        return pieces_of
+
+    def t_copies(block, c, side):
+        return [
+            pltpu.make_async_remote_copy(
+                src_ref=ref, dst_ref=ref,
+                send_sem=t_send.at[side, block], recv_sem=t_recv.at[block, i],
+                device_id={"seq": z + 1 - 2 * side}, device_id_type=MESH,
+            )
+            for ref, i in t_pieces(block, c, side)
+        ]
+
+    def t_arrivals(block, c, side):
+        def wait(ref, i):
+            return lambda: pltpu.make_async_copy(ref, ref, t_recv.at[block, i]).wait()
+
+        return [wait(ref, i) for ref, i in t_pieces(block, c, side)]
 
     def own_tokens(c, do):
         @pl.when(z < n - 1)
         def _():
-            do(t_copy(z, c, 0))
+            for copy in t_copies(z, c, 0):
+                do(copy)
 
         @pl.when(z > 0)
         def _():
-            do(t_copy(z, c, 1))
+            for copy in t_copies(z, c, 1):
+                do(copy)
 
     def own_weights(do):
         for p in range(pieces):
@@ -118,7 +148,7 @@
     def s_copy(block, side):
         return pltpu.make_async_remote_copy(
             src_ref=ss.at[block], dst_ref=ss.at[block],
-            send_sem=s_send.at[side, block], recv_sem=s_recv.at[block],
+            send_sem=s_send.at[0], recv_sem=s_recv.at[block],
             device_id={"seq": z + 1 - 2 * side}, device_id_type=MESH,
         )
 
@@ -159,13 +189,15 @@
     def relay(dist, c):
         @pl.when((z >= dist) & (z < n - 1))
         def _():
-            t_wait(z - dist, c)
-            t_copy(z - dist, c, 0).start()
+            for arrival, copy in zip(t_arrivals(z - dist, c, 0), t_copies(z - dist, c, 0)):
+                arrival()
+                copy.start()
 
         @pl.when((z + dist < n) & (z > 0))
         def _():
-            t_wait(z + dist, c)
-            t_copy(z + dist, c, 1).start()
+            for arrival, copy in zip(t_arrivals(z + dist, c, 1), t_copies(z + dist, c, 1)):
+                arrival()
+                copy.start()
 
     def relay_sums(dist):
         @pl.when((z >= dist) & (z < n - 1))
@@ -178,21 +210,23 @@
             s_wait(z + dist)
             s_copy(z + dist, 1).start()
 
-    def settle(dist, c):
+    def settle(dist, c, piece=0):
         @pl.when((z >= dist) & (z == n - 1))
         def _():
-            t_wait(z - dist, c)
+            t_arrivals(z - dist, c, 0)[piece]()
 
         @pl.when((z + dist < n) & (z == 0))
         def _():
-            t_wait(z + dist, c)
+            t_arrivals(z + dist, c, 1)[piece]()
 
     def token_round(k):
         for dist in range(n - 2, 0, -1):
             c = k - dist + 1
+            if c == chunks - 1 and dist == 1:
+                own_tokens(c, start)
             if 0 <= c < chunks:
                 relay(dist, c)
-        if k + 2 < chunks:
+        if k + 2 < chunks - 1:
             own_tokens(k + 2, start)
 
     rounds = chunks + n - 3
@@ -205,14 +239,14 @@
         if 2 <= step < n:
             relay_sums(step - 1)
         if step < pieces:
-            w_wait(step, xnbr)
+            w_wait(step, 0)
             w_copy(step, 1, 0).start()
 
             @pl.when(core == 1)
             def _():
                 w_copy(step, 1, 2).start()
 
-            w_wait(step, ynbr)
+            w_wait(step, 1)
             w_copy(step, 2, 0).start()
 
             @pl.when(core == 0)
@@ -220,11 +254,9 @@
                 w_copy(step, 2, 1).start()
 
     for p in range(pieces):
-        w_wait(p, diag)
+        w_wait(p, 2)
         w_copy(p, 3, 0).start()
-    for p in range(pieces):
-        for shard in (mate, xnbr + 1 - 2 * core, ynbr + 1 - 2 * core, diag + 1 - 2 * core):
-            w_wait(p, shard)
+    w_bulk(4, w_recv.at[3 * pieces])
     for copy in local:
         copy.wait()
 
@@ -244,8 +276,6 @@
         rows = pl.ds(first, R)
         near = (n - 1) * cols
         left = z == 0
-        near_at = pl.ds(pl.multiple_of(jnp.where(left, 0, cols), 16), near)
-        far_at = pl.ds(pl.multiple_of(jnp.where(left, near, 0), 16), cols)
         for dist in range(1, n):
             @pl.when(left)
             def _():
@@ -256,26 +286,37 @@
                 s_wait(z - dist)
 
         for dist in range(1, n - 1):
-            settle(dist, chunks - 1)
+            for piece in range(2):
+                settle(dist, chunks - 1, piece)
         total = ss[0]
         for s in range(1, n):
             total += ss[s]
         inv = lax.rsqrt(total / (n * cols) + 1e-06)
         inv = jnp.broadcast_to(inv, (R, R)).T[:, :1]
         gain = gain_ref[...]
-        near_gain = jnp.where(left, gain[:, :near], gain[:, cols:])
-        far_gain = jnp.where(left, gain[:, near:], gain[:, :cols])
-        floats = tok[near_at, rows].T.astype(jnp.float32)
-        normed = (floats * inv * near_gain).astype(jnp.bfloat16)
+        some = cols - LATE
+        spans = ((0, cols, near), (near, LATE, some), (near + some, 0, LATE))
+
+        def normed(span):
+            low, high, size = span
+            at = pl.ds(pl.multiple_of(jnp.where(left, low, high), 16), size)
+            scales = jnp.where(left, gain[:, low : low + size], gain[:, high : high + size])
+            floats = tok[at, rows].T.astype(jnp.float32)
+            return (floats * inv * scales).astype(jnp.bfloat16), at
+
+        mine, at = normed(spans[0])
         for p in range(pieces):
-            part_ref[p] = jnp.dot(normed, w[p, near_at, :], preferred_element_type=jnp.float32)
-        settle(n - 1, chunks - 1)
-        floats = tok[far_at, rows].T.astype(jnp.float32)
-        normed = (floats * inv * far_gain).astype(jnp.bfloat16)
+            part_ref[p] = jnp.dot(mine, w[p, at, :], preferred_element_type=jnp.float32)
+        settle(n - 1, chunks - 1, 0)
+        mine, at = normed(spans[1])
+        for p in range(pieces):
+            part_ref[p] += jnp.dot(mine, w[p, at, :], preferred_element_type=jnp.float32)
+        settle(n - 1, chunks - 1, 1)
+        mine, at = normed(spans[2])
         turn = rotate_at(rows)
 
         def project(p):
-            return part_ref[p] + jnp.dot(normed, w[p, far_at, :], preferred_element_type=jnp.float32)
+            return part_ref[p] + jnp.dot(mine, w[p, at, :], preferred_element_type=jnp.float32)
 
         raw = project(0)
         for h in range(kv):
@@ -287,8 +328,8 @@
             raw = project(2 + g)
             for i in range(kv):
                 head = g * kv + i
-                at = (head % groups) * R
-                q_s[head // groups, at : at + R, :] = turn(raw[:, i * HEAD_DIM : (i + 1) * HEAD_DIM])
+                at_q = (head % groups) * R
+                q_s[head // groups, at_q : at_q + R, :] = turn(raw[:, i * HEAD_DIM : (i + 1) * HEAD_DIM])
         row_id = lax.rem(lax.broadcasted_iota(jnp.int32, (groups * R, ROWS), 0), R)
         mask = lax.broadcasted_iota(jnp.int32, (groups * R, ROWS), 1) <= row_id + (ROWS - R)
         for h in range(kv):
@@ -371,7 +412,35 @@
                     sums[:, :HEAD_DIM] / sums[:, HEAD_DIM:]
                 ).astype(jnp.bfloat16)
 
+    def drain_tokens(block, side):
+        sent = tok.at[pl.ds(pl.multiple_of(block * cols, 16), cols), :]
+        pltpu.make_async_copy(sent, sent, t_send.at[side, block]).wait()
+
+    def drain_weights():
+        @pl.when((z == 0) | (z == n - 1))
+        def _():
+            pltpu.make_async_copy(ss.at[pl.ds(0, 1)], ss.at[pl.ds(0, 1)], s_send.at[0]).wait()
+
+        @pl.when((z > 0) & (z < n - 1))
+        def _():
+            sent = ss.at[pl.ds(0, n + 1)]
+            pltpu.make_async_copy(sent, sent, s_send.at[0]).wait()
+
+        w_bulk(7, w_send.at[0])
+
     def body(c, carry):
+        @pl.when(c == 2)
+        def _():
+            drain_weights()
+
+            @pl.when(z == 0)
+            def _():
+                drain_tokens(z, 0)
+
+            @pl.when(z == n - 1)
+            def _():
+                drain_tokens(z, 1)
+
         @pl.when(c == 0)
         def _():
             if early < rounds:
@@ -401,40 +470,18 @@
     def _():
         tail()
 
-
-    own_sums(lambda copy: copy.wait_send())
-    for dist in range(1, n - 1):
-        @pl.when((z >= dist) & (z < n - 1))
-        def _():
-            s_copy(z - dist, 0).wait_send()
-
-        @pl.when((z + dist < n) & (z > 0))
-        def _():
-            s_copy(z + dist, 1).wait_send()
-
-    own_weights(lambda copy: copy.wait_send())
-    for c in range(chunks):
-        own_tokens(c, lambda copy: copy.wait_send())
+    @pl.when((z > 0) & (z < n - 1))
+    def _():
+        for side in range(2):
+            drain_tokens(z, side)
         for dist in range(1, n - 1):
-            @pl.when((z >= dist) & (z < n - 1))
-            def _():
-                t_copy(z - dist, c, 0).wait_send()
-
-            @pl.when((z + dist < n) & (z > 0))
-            def _():
-                t_copy(z + dist, c, 1).wait_send()
-
-    for p in range(pieces):
-        for kind in (1, 2, 3):
-            w_copy(p, kind, 0).wait_send()
-
-        @pl.when(core == 1)
-        def _():
-            w_copy(p, 1, 2).wait_send()
-
-        @pl.when(core == 0)
-        def _():
-            w_copy(p, 2, 1).wait_send()
+            @pl.when(z >= dist)
+            def _():
+                drain_tokens(z - dist, 0)
+
+            @pl.when(z + dist < n)
+            def _():
+                drain_tokens(z + dist, 1)
 
 
 def fused(n, fsdp, tokens, gain, w_query, w_key, w_value):
@@ -468,14 +515,14 @@
             pltpu.VMEM((length, HEAD_DIM), jnp.float32),
             pltpu.VMEM((length, HEAD_DIM), jnp.float32),
             pltpu.VMEM((pieces, WIRE, width), jnp.float32),
-            pltpu.VMEM((n, 1, WIRE), jnp.float32),
+            pltpu.VMEM((n + 1, 1, WIRE), jnp.float32),
             pltpu.SemaphoreType.DMA((3,)),
             pltpu.SemaphoreType.DMA((3 + pieces,)),
-            pltpu.SemaphoreType.DMA((2, n, chunks)),
-            pltpu.SemaphoreType.DMA((n, chunks)),
-            pltpu.SemaphoreType.DMA((3, 4, pieces)),
-            pltpu.SemaphoreType.DMA((fsdp, pieces)),
             pltpu.SemaphoreType.DMA((2, n)),
+            pltpu.SemaphoreType.DMA((n, chunks + 1)),
+            pltpu.SemaphoreType.DMA((1,)),
+            pltpu.SemaphoreType.DMA((3 * pieces + 1,)),
+            pltpu.SemaphoreType.DMA((1,)),
             pltpu.SemaphoreType.DMA((n,)),
         ],
         compiler_params=pltpu.CompilerParams(
@@ -557,6 +604,7 @@
             fsdp == 8
             and n == 4
             and tokens.shape[1] % 16 == 0
+            and tokens.shape[1] > LATE
             and tokens.shape[0] % ROWS == 0
             and tokens.shape[0] >= 3 * ROWS
             and w_key.shape[0] % 16 == 0

time: 86.3 us -> 84.9 us (0.984)
  Pallas kernels: 83.3 us -> 81.9 us
    pallas_call x1, Pallas kernels: 83.3 us -> 81.9 us  [fused(): pl.pallas_call(functools.partial(kernel, n, kv, groups, chunks), out_shap...]
where the time goes in v2:
time: 84.9 us; the launch traced here: 83.2 us
  Pallas kernels  81.9 us (96%)
  local copies, waits for them, and re-layouts  1.32 us (2%)
    pallas_call x1, Pallas kernels, fused(): pl.pallas_call(functools.partial(kernel, n, kv, groups, chunks), out_shap...  81.9 us

profile of v2, /device:TPU:1, one launch (start us, length us, event | category | flops | bytes accessed | tf_op | source)
XLA Modules:
  0.0 83.2 jit_solution(6838098482089457904)
XLA Ops:
  0.0 81.9 %shard_map.73 = bf16[1024,1024]{1,0:T(8,128)(2,1)S(1)} custom-call(bf16[576,1024]{1,0:T(8,128)(2,1)} %bitcast.1, f32[2304]{0:T(1024)} %gain_in.1, f32[1024,128]{1,0:T(8,128)} %constant.4.clone.cos_in, f32[1024,128]{1,0:T(8,128)} %constant.5.clone.sin_in, bf16[288,1024]{1,0:T(8,128)(2,1)} %wq_in.1, bf16[288,512]{1,0:T(8,128)(2,1)} %wk_in.1, ...), custom_call_target="tpu_custom_call" | custom-call | flops 9663676416 | bytes 1179648 | tf_op jit(solution)/shard_map/pallas_call | solution.py:501
  81.9 1.3 %copy.9 = bf16[1024,1024]{1,0:T(8,128)(2,1)} copy(bf16[1024,1024]{1,0:T(8,128)(2,1)S(1)} %shard_map.73) | data formatting | bytes 4194304

commit v3 on v2

--- a/solution.py
+++ b/solution.py
@@ -13,14 +13,16 @@
 ROWS = 256
 WIRE = 128
 LATE = 256
+AHEAD = (6, 1)
+INNER = 2
 MESH = pl.DeviceIdType.MESH
 
 
 def kernel(
     n, kv, groups, chunks,
-    tok_in, gain_in, cos_in, sin_in, wq_in, wk_in, wv_in, out_hbm,
-    tok, w, nrm, q_s, k_s, v_s, acc, gain_ref, cos_ref, sin_ref, part_ref, ss,
-    tok_sem, local_sem, t_send, t_recv, w_send, w_recv, s_send, s_recv,
+    tok_in, gain_in, trig_in, wq_in, wk_in, wv_in, out_hbm,
+    tok, w, nrm, q_s, k_s, v_s, acc, gain_ref, trig_ref, part_ref, ss,
+    tok_sem, local_sem, t_send, t_recv, w_send, w_recv, s_send, s_recv, ready,
 ):
     z = lax.axis_index("seq")
     me = lax.axis_index("fsdp")
@@ -49,19 +51,38 @@
         copy.start()
 
     barrier = pltpu.get_barrier_semaphore()
-    for other in (mate, xnbr, ynbr):
-        pl.semaphore_signal(barrier, inc=1, device_id={"fsdp": other}, device_id_type=MESH)
-
-    @pl.when(z > 0)
+    half = n // 2
+    down = z >= half
+    out = z + 1 - 2 * jnp.where(down, 1, 0)
+    far = z - 1 + 2 * jnp.where(down, 1, 0)
+    outer = (z == 0) | (z == n - 1)
+    links = (
+        ((z < half - 1) | (z > half), ~outer, {"seq": out}, {"seq": far}),
+        (z == half - 1, z == half, {"seq": z + 1}, {"seq": z - 1}),
+        (core == 0, core == 1, {"fsdp": mate}, {"fsdp": mate}),
+        (xpos == 0, xpos == 1, {"fsdp": xnbr}, {"fsdp": xnbr}),
+        (ypos == 0, ypos == 1, {"fsdp": ynbr}, {"fsdp": ynbr}),
+    )
+    for below, _, child, _ in links:
+        @pl.when(below)
+        def _():
+            pl.semaphore_signal(barrier, inc=1, device_id=child, device_id_type=MESH)
+
+    parents = sum(jnp.where(above, 1, 0) for _, above, _, _ in links)
+
+    @pl.when(parents > 0)
     def _():
-        pl.semaphore_signal(barrier, inc=1, device_id={"seq": z - 1}, device_id_type=MESH)
-
-    @pl.when(z < n - 1)
-    def _():
-        pl.semaphore_signal(barrier, inc=1, device_id={"seq": z + 1}, device_id_type=MESH)
-
-    peers = 5 - jnp.where(z == 0, 1, 0) - jnp.where(z == n - 1, 1, 0)
-    pl.semaphore_wait(barrier, peers)
+        pl.semaphore_wait(barrier, parents)
+
+    for i, (_, above, _, parent) in enumerate(links):
+        @pl.when(above)
+        def _():
+            pl.semaphore_signal(ready.at[i], inc=1, device_id=parent, device_id_type=MESH)
+
+    def await_child(i):
+        @pl.when(links[i][0])
+        def _():
+            pl.semaphore_wait(ready.at[i], 1)
 
     def w_own(p):
         if p == 0:
@@ -114,7 +135,7 @@
         return [
             pltpu.make_async_remote_copy(
                 src_ref=ref, dst_ref=ref,
-                send_sem=t_send.at[side, block], recv_sem=t_recv.at[block, i],
+                send_sem=t_send.at[side, block], recv_sem=t_recv.at[block - side, i],
                 device_id={"seq": z + 1 - 2 * side}, device_id_type=MESH,
             )
             for ref, i in t_pieces(block, c, side)
@@ -122,20 +143,9 @@
 
     def t_arrivals(block, c, side):
         def wait(ref, i):
-            return lambda: pltpu.make_async_copy(ref, ref, t_recv.at[block, i]).wait()
+            return lambda: pltpu.make_async_copy(ref, ref, t_recv.at[block - side, i]).wait()
 
         return [wait(ref, i) for ref, i in t_pieces(block, c, side)]
-
-    def own_tokens(c, do):
-        @pl.when(z < n - 1)
-        def _():
-            for copy in t_copies(z, c, 0):
-                do(copy)
-
-        @pl.when(z > 0)
-        def _():
-            for copy in t_copies(z, c, 1):
-                do(copy)
 
     def own_weights(do):
         for p in range(pieces):
@@ -148,12 +158,12 @@
     def s_copy(block, side):
         return pltpu.make_async_remote_copy(
             src_ref=ss.at[block], dst_ref=ss.at[block],
-            send_sem=s_send.at[0], recv_sem=s_recv.at[block],
+            send_sem=s_send.at[0], recv_sem=s_recv.at[block - side],
             device_id={"seq": z + 1 - 2 * side}, device_id_type=MESH,
         )
 
-    def s_wait(block):
-        pltpu.make_async_copy(ss.at[block], ss.at[block], s_recv.at[block]).wait()
+    def s_wait(block, side):
+        pltpu.make_async_copy(ss.at[block], ss.at[block], s_recv.at[block - side]).wait()
 
     def own_sums(do):
         @pl.when(z < n - 1)
@@ -164,25 +174,43 @@
         def _():
             do(s_copy(z, 1))
 
-    def first_tokens():
-        for c in range(2):
+    def own_side(c, side, when):
+        @pl.when(when)
+        def _():
+            for copy in t_copies(z, c, side):
+                copy.start()
+
+    def outward(c, when=True):
+        own_side(c, 1, ~outer & ~down & when)
+        own_side(c, 0, ~outer & down & when)
+
+    def inward(c):
+        own_side(c, 0, ~down)
+        own_side(c, 1, down)
+
+    for c in range(AHEAD[0]):
+        if c < 3:
             loads[c].wait()
-            own_tokens(c, start)
-
-    first_tokens()
-
+        if c < AHEAD[1]:
+            outward(c)
+        else:
+            outward(c, core == 0)
+    for i in (2, 3, 4):
+        await_child(i)
     own_weights(start)
+    await_child(0)
+    await_child(1)
+    for c in range(INNER):
+        inward(c)
     local = []
     for p in range(pieces):
-        local.append(pltpu.make_async_copy(w_own(p), w_slot(p, me), local_sem.at[p]))
-    local.append(pltpu.make_async_copy(gain_in, gain_ref.at[0], local_sem.at[pieces]))
-    local.append(pltpu.make_async_copy(cos_in, cos_ref, local_sem.at[pieces + 1]))
-    local.append(pltpu.make_async_copy(sin_in, sin_ref, local_sem.at[pieces + 2]))
+        local.append(pltpu.make_async_copy(w_own(p), w_slot(p, me), local_sem.at[0]))
+    local.append(pltpu.make_async_copy(gain_in, gain_ref.at[0], local_sem.at[1]))
+    local.append(pltpu.make_async_copy(trig_in, trig_ref, local_sem.at[2]))
     for copy in local:
         copy.start()
     v_s[:, :, HEAD_DIM:] = jnp.ones((kv, v_s.shape[1], HEAD_DIM), jnp.bfloat16)
 
-    loads[2].wait()
     last = t_slot(z, chunks - 1)[...].astype(jnp.float32)
     ss[z] = jnp.sum(last * last, axis=0, keepdims=True)
 
@@ -202,12 +230,12 @@
     def relay_sums(dist):
         @pl.when((z >= dist) & (z < n - 1))
         def _():
-            s_wait(z - dist)
+            s_wait(z - dist, 0)
             s_copy(z - dist, 0).start()
 
         @pl.when((z + dist < n) & (z > 0))
         def _():
-            s_wait(z + dist)
+            s_wait(z + dist, 1)
             s_copy(z + dist, 1).start()
 
     def settle(dist, c, piece=0):
@@ -223,11 +251,15 @@
         for dist in range(n - 2, 0, -1):
             c = k - dist + 1
             if c == chunks - 1 and dist == 1:
-                own_tokens(c, start)
+                outward(c)
+                inward(c)
             if 0 <= c < chunks:
                 relay(dist, c)
-        if k + 2 < chunks - 1:
-            own_tokens(k + 2, start)
+        for side_core in range(2):
+            if k + AHEAD[side_core] < chunks - 1:
+                outward(k + AHEAD[side_core], core == side_core)
+        if k + INNER < chunks - 1:
+            inward(k + INNER)
 
     rounds = chunks + n - 3
     early = min(n + 2, rounds)
@@ -257,7 +289,8 @@
         w_wait(p, 2)
         w_copy(p, 3, 0).start()
     w_bulk(4, w_recv.at[3 * pieces])
-    for copy in local:
+    w_bulk(1, local_sem.at[0])
+    for copy in local[pieces:]:
         copy.wait()
 
     scale = 1.0 / (12.0 * 50.0)
@@ -266,8 +299,8 @@
     R = wire
 
     def rotate_at(rows):
-        cosine = cos_ref[rows, :]
-        sine = sin_ref[rows, :]
+        cosine = trig_ref[0, rows, :]
+        sine = trig_ref[1, rows, :]
         return lambda x: (x * cosine + pltpu.roll(x, HEAD_DIM // 2, 1) * sine).astype(jnp.bfloat16)
 
     def tail():
@@ -279,11 +312,11 @@
         for dist in range(1, n):
             @pl.when(left)
             def _():
-                s_wait(z + dist)
+                s_wait(z + dist, 1)
 
             @pl.when(z == n - 1)
             def _():
-                s_wait(z - dist)
+                s_wait(z - dist, 0)
 
         for dist in range(1, n - 1):
             for piece in range(2):
@@ -501,7 +534,7 @@
     return pl.pallas_call(
         functools.partial(kernel, n, kv, groups, chunks),
         out_shape=pltpu.VMEM((length, w_query.shape[1]), jnp.bfloat16),
-        in_specs=[hbm] * 7,
+        in_specs=[hbm] * 6,
         out_specs=pl.BlockSpec(memory_space=pltpu.VMEM),
         scratch_shapes=[
             pltpu.VMEM((n * cols, length), jnp.bfloat16),
@@ -512,24 +545,24 @@
             pltpu.VMEM((kv, length, 2 * HEAD_DIM), jnp.bfloat16),
             pltpu.VMEM((kv, groups * WIRE, 2 * HEAD_DIM), jnp.float32),
             pltpu.VMEM((1, n * cols), jnp.float32),
-            pltpu.VMEM((length, HEAD_DIM), jnp.float32),
-            pltpu.VMEM((length, HEAD_DIM), jnp.float32),
+            pltpu.VMEM((2, length, HEAD_DIM), jnp.float32),
             pltpu.VMEM((pieces, WIRE, width), jnp.float32),
             pltpu.VMEM((n + 1, 1, WIRE), jnp.float32),
             pltpu.SemaphoreType.DMA((3,)),
-            pltpu.SemaphoreType.DMA((3 + pieces,)),
+            pltpu.SemaphoreType.DMA((3,)),
             pltpu.SemaphoreType.DMA((2, n)),
-            pltpu.SemaphoreType.DMA((n, chunks + 1)),
+            pltpu.SemaphoreType.DMA((n - 1, chunks + 1)),
             pltpu.SemaphoreType.DMA((1,)),
             pltpu.SemaphoreType.DMA((3 * pieces + 1,)),
             pltpu.SemaphoreType.DMA((1,)),
-            pltpu.SemaphoreType.DMA((n,)),
+            pltpu.SemaphoreType.DMA((n - 1,)),
+            pltpu.SemaphoreType.REGULAR((5,)),
         ],
         compiler_params=pltpu.CompilerParams(
             collective_id=0, has_side_effects=True, vmem_limit_bytes=60 * 1024 * 1024
         ),
         cost_estimate=pl.CostEstimate(flops=flops, bytes_accessed=2 * length * cols, transcendentals=0),
-    )(tokens.T, gain, jnp.asarray(cosine), jnp.asarray(sine), w_query, w_key, w_value)
+    )(tokens.T, gain, jnp.asarray(np.stack([cosine, sine])), w_query, w_key, w_value)
 
 
 def rotate(values, positions):

time: 84.9 us -> 83.7 us (0.986); the launches traced: 83.2 us -> 83.6 us
  no operation moved by 1% of the time
where the time goes in v3:
time: 83.7 us; the launch traced here: 83.6 us
  Pallas kernels  82.3 us (98%)
  local copies, waits for them, and re-layouts  1.32 us (2%)
    pallas_call x1, Pallas kernels, fused(): pl.pallas_call(functools.partial(kernel, n, kv, groups, chunks), out_shap...  82.3 us

profile of v3, /device:TPU:1, one launch (start us, length us, event | category | flops | bytes accessed | tf_op | source)
XLA Modules:
  0.0 83.6 jit_solution(13198036253964980208)
XLA Ops:
  0.0 82.3 %shard_map.64 = bf16[1024,1024]{1,0:T(8,128)(2,1)S(1)} custom-call(bf16[576,1024]{1,0:T(8,128)(2,1)} %bitcast.1, f32[2304]{0:T(1024)} %gain_in.1, f32[2,1024,128]{2,1,0:T(8,128)} %constant.2.clone.trig_in, bf16[288,1024]{1,0:T(8,128)(2,1)} %wq_in.1, bf16[288,512]{1,0:T(8,128)(2,1)} %wk_in.1, bf16[288,512]{1,0:T(8,128)(2,1)} %wv_in.1), custom_call_target="tpu_custom_call" | custom-call | flops 9663676416 | bytes 1179648 | tf_op jit(solution)/shard_map/pallas_call | solution.py:534
  82.3 1.3 %copy.8 = bf16[1024,1024]{1,0:T(8,128)(2,1)} copy(bf16[1024,1024]{1,0:T(8,128)(2,1)S(1)} %shard_map.64) | data formatting | bytes 4194304

commit v4 on v3

--- a/solution.py
+++ b/solution.py
@@ -15,13 +15,14 @@
 LATE = 256
 AHEAD = (6, 1)
 INNER = 2
+FIRST = 2
 MESH = pl.DeviceIdType.MESH
 
 
 def kernel(
     n, kv, groups, chunks,
-    tok_in, gain_in, trig_in, wq_in, wk_in, wv_in, out_hbm,
-    tok, w, nrm, q_s, k_s, v_s, acc, gain_ref, trig_ref, part_ref, ss,
+    tok_in, gain_in, trig_in, wq_in, wk_in, wv_in, out_ref, q_s, k_s, v_s,
+    tok, w, nrm, acc, gain_ref, trig_ref, part_ref, ss,
     tok_sem, local_sem, t_send, t_recv, w_send, w_recv, s_send, s_recv, ready,
 ):
     z = lax.axis_index("seq")
@@ -184,9 +185,9 @@
         own_side(c, 1, ~outer & ~down & when)
         own_side(c, 0, ~outer & down & when)
 
-    def inward(c):
-        own_side(c, 0, ~down)
-        own_side(c, 1, down)
+    def inward(c, when=True):
+        own_side(c, 0, ~down & when)
+        own_side(c, 1, down & when)
 
     for c in range(AHEAD[0]):
         if c < 3:
@@ -202,6 +203,8 @@
     await_child(1)
     for c in range(INNER):
         inward(c)
+    for c in range(INNER, chunks):
+        inward(c, outer)
     local = []
     for p in range(pieces):
         local.append(pltpu.make_async_copy(w_own(p), w_slot(p, me), local_sem.at[0]))
@@ -252,14 +255,13 @@
             c = k - dist + 1
             if c == chunks - 1 and dist == 1:
                 outward(c)
-                inward(c)
             if 0 <= c < chunks:
                 relay(dist, c)
         for side_core in range(2):
             if k + AHEAD[side_core] < chunks - 1:
                 outward(k + AHEAD[side_core], core == side_core)
-        if k + INNER < chunks - 1:
-            inward(k + INNER)
+        if k + INNER < chunks:
+            inward(k + INNER, ~outer)
 
     rounds = chunks + n - 3
     early = min(n + 2, rounds)
@@ -363,26 +365,39 @@
                 head = g * kv + i
                 at_q = (head % groups) * R
                 q_s[head // groups, at_q : at_q + R, :] = turn(raw[:, i * HEAD_DIM : (i + 1) * HEAD_DIM])
-        row_id = lax.rem(lax.broadcasted_iota(jnp.int32, (groups * R, ROWS), 0), R)
-        mask = lax.broadcasted_iota(jnp.int32, (groups * R, ROWS), 1) <= row_id + (ROWS - R)
+
+    def attend(rows, low, last, base_count):
+        def block(h, keys, mask):
+            s = lax.dot_general(
+                q_s[h, : groups * R, :], k_s[h, keys, :], (((1,), (1,)), ((), ())),
+                preferred_element_type=jnp.float32,
+            )
+            e = jnp.exp2(jnp.tanh(s * scale) * peak)
+            if mask is not None:
+                e = jnp.where(mask, e, 0.0)
+            return jnp.dot(
+                e.astype(jnp.bfloat16), v_s[h, keys, :], preferred_element_type=jnp.float32
+            )
+
+        row_id = lax.rem(lax.broadcasted_iota(jnp.int32, (groups * R, last), 0), R)
+        mask = lax.broadcasted_iota(jnp.int32, (groups * R, last), 1) <= row_id + (last - R)
+        top = pl.ds(low, last)
         for h in range(kv):
-            sums = None
-            for low in range(0, length, ROWS):
-                keys = pl.ds(low, ROWS)
-                s = lax.dot_general(
-                    q_s[h, : groups * R, :], k_s[h, keys, :], (((1,), (1,)), ((), ())),
-                    preferred_element_type=jnp.float32,
-                )
-                e = jnp.exp2(jnp.tanh(s * scale) * peak)
-                if low + ROWS == length:
-                    e = jnp.where(mask, e, 0.0)
-                e = jnp.dot(e.astype(jnp.bfloat16), v_s[h, keys, :], preferred_element_type=jnp.float32)
-                sums = e if sums is None else sums + e
+            acc[h, : groups * R, :] = block(h, top, mask)
+
+        def inner(j, carry):
+            keys = pl.ds(pl.multiple_of(j * ROWS, ROWS), ROWS)
+            for h in range(kv):
+                acc[h, : groups * R, :] += block(h, keys, None)
+            return carry
+
+        lax.fori_loop(0, base_count, inner, 0)
+        for h in range(kv):
             for g in range(groups):
+                sums = acc[h, g * R : (g + 1) * R, :]
                 head = h * groups + g
-                part = sums[g * R : (g + 1) * R, :]
-                out_hbm[rows, head * HEAD_DIM : (head + 1) * HEAD_DIM] = (
-                    part[:, :HEAD_DIM] / part[:, HEAD_DIM:]
+                out_ref[rows, head * HEAD_DIM : (head + 1) * HEAD_DIM] = (
+                    sums[:, :HEAD_DIM] / sums[:, HEAD_DIM:]
                 ).astype(jnp.bfloat16)
 
     def chunk(first, low, last, base_count, part):
@@ -412,38 +427,9 @@
                     raw[:, i * HEAD_DIM : (i + 1) * HEAD_DIM]
                 )
 
-        def block(h, keys, mask):
-            s = lax.dot_general(
-                q_s[h, : groups * R, :], k_s[h, keys, :], (((1,), (1,)), ((), ())),
-                preferred_element_type=jnp.float32,
-            )
-            e = jnp.exp2(jnp.tanh(s * scale) * peak)
-            if mask is not None:
-                e = jnp.where(mask, e, 0.0)
-            return jnp.dot(
-                e.astype(jnp.bfloat16), v_s[h, keys, :], preferred_element_type=jnp.float32
-            )
-
-        row_id = lax.rem(lax.broadcasted_iota(jnp.int32, (groups * R, last), 0), R)
-        mask = lax.broadcasted_iota(jnp.int32, (groups * R, last), 1) <= row_id + (last - R)
-        top = pl.ds(low, last)
-        for h in range(kv):
-            acc[h, : groups * R, :] = block(h, top, mask)
-
-        def inner(j, carry):
-            keys = pl.ds(pl.multiple_of(j * ROWS, ROWS), ROWS)
-            for h in range(kv):
-                acc[h, : groups * R, :] += block(h, keys, None)
-            return carry
-
-        lax.fori_loop(0, base_count, inner, 0)
-        for h in range(kv):
-            for g in range(groups):
-                sums = acc[h, g * R : (g + 1) * R, :]
-                head = h * groups + g
-                out_hbm[rows, head * HEAD_DIM : (head + 1) * HEAD_DIM] = (
-                    sums[:, :HEAD_DIM] / sums[:, HEAD_DIM:]
-                ).astype(jnp.bfloat16)
+        @pl.when(part < chunks - 1)
+        def _():
+            attend(rows, low, last, base_count)
 
     def drain_tokens(block, side):
         sent = tok.at[pl.ds(pl.multiple_of(block * cols, 16), cols), :]
@@ -473,22 +459,19 @@
             @pl.when(z == n - 1)
             def _():
                 drain_tokens(z, 1)
-
-        @pl.when(c == 0)
-        def _():
-            if early < rounds:
-                token_round(early)
-
-        @pl.when(c == 1)
-        def _():
-            for k in range(early + 1, rounds):
-                token_round(k)
 
         low = pl.multiple_of(c * ROWS, ROWS)
         per = ROWS // R
         for i in range(per):
             first = pl.multiple_of(c * ROWS + i * R, R)
             part = c * per + i
+            for k in range(early, rounds):
+                before = 0 if k == early else FIRST + k - early - 1
+                if before % per == i:
+                    @pl.when(c == before // per)
+                    def _():
+                        token_round(k)
+
             if i < per - 1:
                 chunk(first, low, (i + 1) * R, c, part)
             else:
@@ -515,6 +498,46 @@
             @pl.when(z + dist < n)
             def _():
                 drain_tokens(z + dist, 1)
+
+
+def finish(out_ref, q_s, k_s, v_s, out_hbm, last_ref, sems):
+    length, width = out_ref.shape
+    kv, tall = q_s.shape[:2]
+    groups = tall // WIRE
+    R = WIRE
+    first = length - R
+    scale = 1.0 / (12.0 * 50.0)
+    peak = 50.0 * math.log2(math.e)
+    done = pl.ds(0, first)
+    copies = [pltpu.make_async_copy(out_ref.at[done, :], out_hbm.at[done, :], sems.at[0])]
+    copies[0].start()
+    rows = pl.ds(first, R)
+    row_id = lax.rem(lax.broadcasted_iota(jnp.int32, (groups * R, ROWS), 0), R)
+    mask = lax.broadcasted_iota(jnp.int32, (groups * R, ROWS), 1) <= row_id + (ROWS - R)
+    for h in range(kv):
+        sums = None
+        for low in range(0, length, ROWS):
+            keys = pl.ds(low, ROWS)
+            s = lax.dot_general(
+                q_s[h, : groups * R, :], k_s[h, keys, :], (((1,), (1,)), ((), ())),
+                preferred_element_type=jnp.float32,
+            )
+            e = jnp.exp2(jnp.tanh(s * scale) * peak)
+            if low + ROWS == length:
+                e = jnp.where(mask, e, 0.0)
+            e = jnp.dot(e.astype(jnp.bfloat16), v_s[h, keys, :], preferred_element_type=jnp.float32)
+            sums = e if sums is None else sums + e
+        for g in range(groups):
+            head = h * groups + g
+            part = sums[g * R : (g + 1) * R, :]
+            last_ref[:, head * HEAD_DIM : (head + 1) * HEAD_DIM] = (
+                part[:, :HEAD_DIM] / part[:, HEAD_DIM:]
+            ).astype(jnp.bfloat16)
+        lanes = pl.ds(h * groups * HEAD_DIM, groups * HEAD_DIM)
+        copies.append(pltpu.make_async_copy(last_ref.at[:, lanes], out_hbm.at[rows, lanes], sems.at[1 + h]))
+        copies[-1].start()
+    for copy in copies:
+        copy.wait()
 
 
 def fused(n, fsdp, tokens, gain, w_query, w_key, w_value):
@@ -531,18 +554,22 @@
     hbm = pl.BlockSpec(memory_space=pl.ANY)
     pieces = 2 + groups
     flops = 2 * length * fsdp * depth * width * pieces
-    return pl.pallas_call(
+    vmem = pl.BlockSpec(memory_space=pltpu.VMEM)
+    heads = w_query.shape[1]
+    state = pl.pallas_call(
         functools.partial(kernel, n, kv, groups, chunks),
-        out_shape=pltpu.VMEM((length, w_query.shape[1]), jnp.bfloat16),
+        out_shape=(
+            pltpu.VMEM((length, heads), jnp.bfloat16),
+            pltpu.VMEM((kv, groups * WIRE, HEAD_DIM), jnp.bfloat16),
+            pltpu.VMEM((kv, length, HEAD_DIM), jnp.bfloat16),
+            pltpu.VMEM((kv, length, 2 * HEAD_DIM), jnp.bfloat16),
+        ),
         in_specs=[hbm] * 6,
-        out_specs=pl.BlockSpec(memory_space=pltpu.VMEM),
+        out_specs=[vmem] * 4,
         scratch_shapes=[
             pltpu.VMEM((n * cols, length), jnp.bfloat16),
             pltpu.VMEM((pieces, fsdp * depth, width), jnp.bfloat16),
             pltpu.VMEM((WIRE, n * cols), jnp.bfloat16),
-            pltpu.VMEM((kv, groups * WIRE, HEAD_DIM), jnp.bfloat16),
-            pltpu.VMEM((kv, length, HEAD_DIM), jnp.bfloat16),
-            pltpu.VMEM((kv, length, 2 * HEAD_DIM), jnp.bfloat16),
             pltpu.VMEM((kv, groups * WIRE, 2 * HEAD_DIM), jnp.float32),
             pltpu.VMEM((1, n * cols), jnp.float32),
             pltpu.VMEM((2, length, HEAD_DIM), jnp.float32),
@@ -559,10 +586,18 @@
             pltpu.SemaphoreType.REGULAR((5,)),
         ],
         compiler_params=pltpu.CompilerParams(
-            collective_id=0, has_side_effects=True, vmem_limit_bytes=60 * 1024 * 1024
+            collective_id=0, has_side_effects=True, vmem_limit_bytes=58 * 1024 * 1024
         ),
         cost_estimate=pl.CostEstimate(flops=flops, bytes_accessed=2 * length * cols, transcendentals=0),
     )(tokens.T, gain, jnp.asarray(np.stack([cosine, sine])), w_query, w_key, w_value)
+    return pl.pallas_call(
+        finish,
+        out_shape=jax.ShapeDtypeStruct((length, heads), jnp.bfloat16),
+        in_specs=[vmem] * 4,
+        out_specs=hbm,
+        scratch_shapes=[pltpu.VMEM((WIRE, heads), jnp.bfloat16), pltpu.SemaphoreType.DMA((1 + kv,))],
+        compiler_params=pltpu.CompilerParams(vmem_limit_bytes=16 * 1024 * 1024),
+    )(*(pltpu.with_memory_space_constraint(x, pltpu.VMEM) for x in state))
 
 
 def rotate(values, positions):

time: 83.7 us -> 83.2 us (level)
  local copies, waits for them, and re-layouts: 1.32 us -> 0 us
    pallas_call x0 -> x1, Pallas kernels: none -> 2.17 us  [fused(): pl.pallas_call(finish, out_shape=jax.ShapeDtypeStruct((length, heads), jn...]
    pallas_call x1, Pallas kernels: 82.3 us -> 80.9 us  [fused(): pl.pallas_call(functools.partial(kernel, n, kv, groups, chunks), out_shap...]
    unnamed x1 -> x0, local copies, waits for them, and re-layouts: 1.32 us -> none
where the time goes in v4:
time: 83.2 us; the launch traced here: 83.1 us
  Pallas kernels  83.1 us (100%)
    pallas_call x1, Pallas kernels, fused(): pl.pallas_call(functools.partial(kernel, n, kv, groups, chunks), out_shap...  80.9 us
    pallas_call x1, Pallas kernels, fused(): pl.pallas_call(finish, out_shape=jax.ShapeDtypeStruct((length, heads), jn...  2.17 us

profile of v4, /device:TPU:1, one launch (start us, length us, event | category | flops | bytes accessed | tf_op | source)
XLA Modules:
  0.0 83.1 jit_solution(7053565593578835092)
XLA Ops:
  0.0 80.9 %shard_map.64 = (bf16[1024,1024]{1,0:T(8,128)(2,1)S(1)}, bf16[4,256,128]{2,1,0:T(8,128)(2,1)S(1)}, bf16[4,1024,128]{2,1,0:T(8,128)(2,1)S(1)}, bf16[4,1024,256]{2,1,0:T(8,128)(2,1)S(1)}) custom-call(bf16[576,1024]{1,0:T(8,128)(2,1)} %bitcast.1, f32[2304]{0:T(1024)} %gain_in.1, f32[2,1024,128]{2,1,0:T(8,128)} %constant.2.clone.trig_in, ...), custom_call_target="tpu_custom_call" | custom-call | flops 9663676416 | bytes 1179648 | tf_op jit(solution)/shard_map/pallas_call | solution.py:559
  80.9 2.2 %shard_map.65 = bf16[1024,1024]{1,0:T(8,128)(2,1)} custom-call(bf16[1024,1024]{1,0:T(8,128)(2,1)S(1)} %get-tuple-element.9.out_ref, bf16[4,256,128]{2,1,0:T(8,128)(2,1)S(1)} %get-tuple-element.10.q_s, bf16[4,1024,128]{2,1,0:T(8,128)(2,1)S(1)} %get-tuple-element.11.k_s, bf16[4,1024,256]{2,1,0:T(8,128)(2,1)S(1)} %get-tuple-element.12.v_s), custom_call_target="tpu_custom_call" | custom-call | tf_op jit(solution)/shard_map/pallas_call | solution.py:593

commit v5 on v4

--- a/solution.py
+++ b/solution.py
@@ -13,9 +13,10 @@
 ROWS = 256
 WIRE = 128
 LATE = 256
-AHEAD = (6, 1)
+AHEAD = (5, 1)
 INNER = 2
 FIRST = 2
+DIRECT = 1
 MESH = pl.DeviceIdType.MESH
 
 
@@ -78,12 +79,12 @@
     for i, (_, above, _, parent) in enumerate(links):
         @pl.when(above)
         def _():
-            pl.semaphore_signal(ready.at[i], inc=1, device_id=parent, device_id_type=MESH)
+            pl.semaphore_signal(ready.at[max(i - 1, 0)], inc=1, device_id=parent, device_id_type=MESH)
 
     def await_child(i):
         @pl.when(links[i][0])
         def _():
-            pl.semaphore_wait(ready.at[i], 1)
+            pl.semaphore_wait(ready.at[max(i - 1, 0)], 1)
 
     def w_own(p):
         if p == 0:
@@ -95,10 +96,13 @@
     def w_slot(p, f):
         return w.at[p, pl.ds(pl.multiple_of(f * depth, 16), depth), :]
 
+    pair = 2 if pieces % 2 == 0 else 1
+    sets = pieces // pair
+
     def w_mark(p, kind, lane):
         if lane == 0:
-            return w_recv.at[3 * pieces]
-        return w_recv.at[(lane - 1 if kind == 0 else 2) * pieces + p]
+            return w_recv.at[2 * sets + 1]
+        return w_recv.at[(lane - 1) * sets + p // pair if kind == 0 else 2 * sets]
 
     def w_copy(p, kind, lane):
         shard = (me, xnbr, ynbr, diag)[kind]
@@ -109,9 +113,10 @@
             device_id={"fsdp": (mate, xnbr, ynbr)[lane]}, device_id_type=MESH,
         )
 
-    def w_wait(p, i):
-        slot = w_slot(p, (xnbr, ynbr, diag)[i])
-        pltpu.make_async_copy(slot, slot, w_recv.at[i * pieces + p]).wait()
+    def w_wait(first, count, shard, sem):
+        rows = pl.ds(pl.multiple_of(shard * depth, 16), depth)
+        slots = w.at[pl.ds(first, count), rows, :]
+        pltpu.make_async_copy(slots, slots, sem).wait()
 
     def w_bulk(count, sem):
         slots = w.at[:, pl.ds(0, count * depth), :]
@@ -132,11 +137,11 @@
             pieces_of.append((tok.at[rows, lanes], i))
         return pieces_of
 
-    def t_copies(block, c, side):
+    def t_copies(block, c, side, direct=False, hop=0):
         return [
             pltpu.make_async_remote_copy(
-                src_ref=ref, dst_ref=ref,
-                send_sem=t_send.at[side, block], recv_sem=t_recv.at[block - side, i],
+                src_ref=tok_in.at[:, pl.ds(c * wire, wire)] if direct else ref, dst_ref=ref,
+                send_sem=t_send.at[2 * hop + side], recv_sem=t_recv.at[block - side, i],
                 device_id={"seq": z + 1 - 2 * side}, device_id_type=MESH,
             )
             for ref, i in t_pieces(block, c, side)
@@ -175,27 +180,28 @@
         def _():
             do(s_copy(z, 1))
 
-    def own_side(c, side, when):
+    def own_side(c, side, when, direct=False):
         @pl.when(when)
         def _():
-            for copy in t_copies(z, c, side):
+            for copy in t_copies(z, c, side, direct):
                 copy.start()
 
-    def outward(c, when=True):
-        own_side(c, 1, ~outer & ~down & when)
-        own_side(c, 0, ~outer & down & when)
+    def outward(c, when=True, direct=False):
+        own_side(c, 1, ~outer & ~down & when, direct)
+        own_side(c, 0, ~outer & down & when, direct)
 
     def inward(c, when=True):
         own_side(c, 0, ~down & when)
         own_side(c, 1, down & when)
 
     for c in range(AHEAD[0]):
-        if c < 3:
-            loads[c].wait()
-        if c < AHEAD[1]:
-            outward(c)
-        else:
-            outward(c, core == 0)
+        direct = c < DIRECT
+        if not direct:
+            for i in range(DIRECT + 1 if c == DIRECT else 0):
+                loads[i].wait()
+            if DIRECT < c < 3:
+                loads[c].wait()
+        outward(c, True if c < AHEAD[1] else core == 0, direct)
     for i in (2, 3, 4):
         await_child(i)
     own_weights(start)
@@ -220,13 +226,13 @@
     def relay(dist, c):
         @pl.when((z >= dist) & (z < n - 1))
         def _():
-            for arrival, copy in zip(t_arrivals(z - dist, c, 0), t_copies(z - dist, c, 0)):
+            for arrival, copy in zip(t_arrivals(z - dist, c, 0), t_copies(z - dist, c, 0, hop=dist)):
                 arrival()
                 copy.start()
 
         @pl.when((z + dist < n) & (z > 0))
         def _():
-            for arrival, copy in zip(t_arrivals(z + dist, c, 1), t_copies(z + dist, c, 1)):
+            for arrival, copy in zip(t_arrivals(z + dist, c, 1), t_copies(z + dist, c, 1, hop=dist)):
                 arrival()
                 copy.start()
 
@@ -272,25 +278,30 @@
             own_sums(start)
         if 2 <= step < n:
             relay_sums(step - 1)
-        if step < pieces:
-            w_wait(step, 0)
-            w_copy(step, 1, 0).start()
+        if step < pieces and step % pair == pair - 1:
+            group = range(step + 1 - pair, step + 1)
+            w_wait(group[0], pair, xnbr, w_recv.at[step // pair])
+            for p in group:
+                w_copy(p, 1, 0).start()
 
             @pl.when(core == 1)
             def _():
-                w_copy(step, 1, 2).start()
-
-            w_wait(step, 1)
-            w_copy(step, 2, 0).start()
+                for p in group:
+                    w_copy(p, 1, 2).start()
+
+            w_wait(group[0], pair, ynbr, w_recv.at[sets + step // pair])
+            for p in group:
+                w_copy(p, 2, 0).start()
 
             @pl.when(core == 0)
             def _():
-                w_copy(step, 2, 1).start()
-
+                for p in group:
+                    w_copy(p, 2, 1).start()
+
+    w_wait(0, pieces, diag, w_recv.at[2 * sets])
     for p in range(pieces):
-        w_wait(p, 2)
         w_copy(p, 3, 0).start()
-    w_bulk(4, w_recv.at[3 * pieces])
+    w_bulk(4, w_recv.at[2 * sets + 1])
     w_bulk(1, local_sem.at[0])
     for copy in local[pieces:]:
         copy.wait()
@@ -431,9 +442,9 @@
         def _():
             attend(rows, low, last, base_count)
 
-    def drain_tokens(block, side):
+    def drain_tokens(block, side, hop=0):
         sent = tok.at[pl.ds(pl.multiple_of(block * cols, 16), cols), :]
-        pltpu.make_async_copy(sent, sent, t_send.at[side, block]).wait()
+        pltpu.make_async_copy(sent, sent, t_send.at[2 * hop + side]).wait()
 
     def drain_weights():
         @pl.when((z == 0) | (z == n - 1))
@@ -493,11 +504,11 @@
         for dist in range(1, n - 1):
             @pl.when(z >= dist)
             def _():
-                drain_tokens(z - dist, 0)
+                drain_tokens(z - dist, 0, dist)
 
             @pl.when(z + dist < n)
             def _():
-                drain_tokens(z + dist, 1)
+                drain_tokens(z + dist, 1, dist)
 
 
 def finish(out_ref, q_s, k_s, v_s, out_hbm, last_ref, sems):
@@ -577,13 +588,13 @@
             pltpu.VMEM((n + 1, 1, WIRE), jnp.float32),
             pltpu.SemaphoreType.DMA((3,)),
             pltpu.SemaphoreType.DMA((3,)),
-            pltpu.SemaphoreType.DMA((2, n)),
+            pltpu.SemaphoreType.DMA((2 * (n - 1),)),
             pltpu.SemaphoreType.DMA((n - 1, chunks + 1)),
             pltpu.SemaphoreType.DMA((1,)),
-            pltpu.SemaphoreType.DMA((3 * pieces + 1,)),
+            pltpu.SemaphoreType.DMA((2 * (pieces // 2 if pieces % 2 == 0 else pieces) + 2,)),
             pltpu.SemaphoreType.DMA((1,)),
             pltpu.SemaphoreType.DMA((n - 1,)),
-            pltpu.SemaphoreType.REGULAR((5,)),
+            pltpu.SemaphoreType.REGULAR((4,)),
         ],
         compiler_params=pltpu.CompilerParams(
             collective_id=0, has_side_effects=True, vmem_limit_bytes=58 * 1024 * 1024

time: 83.2 us -> 83.1 us (level)
  no operation moved by 1% of the time
where the time goes in v5:
time: 83.1 us; the launch traced here: 83 us
  Pallas kernels  83 us (100%)
    pallas_call x1, Pallas kernels, fused(): pl.pallas_call(functools.partial(kernel, n, kv, groups, chunks), out_shap...  80.8 us
    pallas_call x1, Pallas kernels, fused(): pl.pallas_call(finish, out_shape=jax.ShapeDtypeStruct((length, heads), jn...  2.17 us

profile of v5, /device:TPU:1, one launch (start us, length us, event | category | flops | bytes accessed | tf_op | source)
XLA Modules:
  0.0 83.0 jit_solution(15337309342468508412)
XLA Ops:
  0.0 80.8 %shard_map.64 = (bf16[1024,1024]{1,0:T(8,128)(2,1)S(1)}, bf16[4,256,128]{2,1,0:T(8,128)(2,1)S(1)}, bf16[4,1024,128]{2,1,0:T(8,128)(2,1)S(1)}, bf16[4,1024,256]{2,1,0:T(8,128)(2,1)S(1)}) custom-call(bf16[576,1024]{1,0:T(8,128)(2,1)} %bitcast.1, f32[2304]{0:T(1024)} %gain_in.1, f32[2,1024,128]{2,1,0:T(8,128)} %constant.2.clone.trig_in, ...), custom_call_target="tpu_custom_call" | custom-call | flops 9663676416 | bytes 1179648 | tf_op jit(solution)/shard_map/pallas_call | solution.py:570
  80.8 2.2 %shard_map.65 = bf16[1024,1024]{1,0:T(8,128)(2,1)} custom-call(bf16[1024,1024]{1,0:T(8,128)(2,1)S(1)} %get-tuple-element.9.out_ref, bf16[4,256,128]{2,1,0:T(8,128)(2,1)S(1)} %get-tuple-element.10.q_s, bf16[4,1024,128]{2,1,0:T(8,128)(2,1)S(1)} %get-tuple-element.11.k_s, bf16[4,1024,256]{2,1,0:T(8,128)(2,1)S(1)} %get-tuple-element.12.v_s), custom_call_target="tpu_custom_call" | custom-call | tf_op jit(solution)/shard_map/pallas_call | solution.py:604

commit v6 on v5

--- a/solution.py
+++ b/solution.py
@@ -274,10 +274,10 @@
     for step in range(max(early, pieces)):
         if step < early:
             token_round(step)
-        if step == 1:
+        if step == 2:
             own_sums(start)
-        if 2 <= step < n:
-            relay_sums(step - 1)
+        if 3 <= step <= n:
+            relay_sums(step - 2)
         if step < pieces and step % pair == pair - 1:
             group = range(step + 1 - pair, step + 1)
             w_wait(group[0], pair, xnbr, w_recv.at[step // pair])
@@ -527,7 +527,7 @@
     mask = lax.broadcasted_iota(jnp.int32, (groups * R, ROWS), 1) <= row_id + (ROWS - R)
     for h in range(kv):
         sums = None
-        for low in range(0, length, ROWS):
+        for low in range(length - ROWS, -1, -ROWS):
             keys = pl.ds(low, ROWS)
             s = lax.dot_general(
                 q_s[h, : groups * R, :], k_s[h, keys, :], (((1,), (1,)), ((), ())),

time: 83.1 us -> 83.1 us (level)
  no operation moved by 1% of the time
where the time goes in v6:
time: 83.1 us; the launch traced here: 83 us
  Pallas kernels  83 us (100%)
    pallas_call x1, Pallas kernels, fused(): pl.pallas_call(functools.partial(kernel, n, kv, groups, chunks), out_shap...  80.8 us
    pallas_call x1, Pallas kernels, fused(): pl.pallas_call(finish, out_shape=jax.ShapeDtypeStruct((length, heads), jn...  2.18 us

profile of v6, /device:TPU:1, one launch (start us, length us, event | category | flops | bytes accessed | tf_op | source)
XLA Modules:
  0.0 83.0 jit_solution(5641913074525042117)
XLA Ops:
  0.0 80.8 %shard_map.64 = (bf16[1024,1024]{1,0:T(8,128)(2,1)S(1)}, bf16[4,256,128]{2,1,0:T(8,128)(2,1)S(1)}, bf16[4,1024,128]{2,1,0:T(8,128)(2,1)S(1)}, bf16[4,1024,256]{2,1,0:T(8,128)(2,1)S(1)}) custom-call(bf16[576,1024]{1,0:T(8,128)(2,1)} %bitcast.1, f32[2304]{0:T(1024)} %gain_in.1, f32[2,1024,128]{2,1,0:T(8,128)} %constant.2.clone.trig_in, ...), custom_call_target="tpu_custom_call" | custom-call | flops 9663676416 | bytes 1179648 | tf_op jit(solution)/shard_map/pallas_call | solution.py:570
  80.8 2.2 %shard_map.65 = bf16[1024,1024]{1,0:T(8,128)(2,1)} custom-call(bf16[1024,1024]{1,0:T(8,128)(2,1)S(1)} %get-tuple-element.9.out_ref, bf16[4,256,128]{2,1,0:T(8,128)(2,1)S(1)} %get-tuple-element.10.q_s, bf16[4,1024,128]{2,1,0:T(8,128)(2,1)S(1)} %get-tuple-element.11.k_s, bf16[4,1024,256]{2,1,0:T(8,128)(2,1)S(1)} %get-tuple-element.12.v_s), custom_call_target="tpu_custom_call" | custom-call | tf_op jit(solution)/shard_map/pallas_call | solution.py:604

commit v7 on v6

--- a/solution.py
+++ b/solution.py
@@ -96,7 +96,7 @@
     def w_slot(p, f):
         return w.at[p, pl.ds(pl.multiple_of(f * depth, 16), depth), :]
 
-    pair = 2 if pieces % 2 == 0 else 1
+    pair = pieces
     sets = pieces // pair
 
     def w_mark(p, kind, lane):
@@ -591,7 +591,7 @@
             pltpu.SemaphoreType.DMA((2 * (n - 1),)),
             pltpu.SemaphoreType.DMA((n - 1, chunks + 1)),
             pltpu.SemaphoreType.DMA((1,)),
-            pltpu.SemaphoreType.DMA((2 * (pieces // 2 if pieces % 2 == 0 else pieces) + 2,)),
+            pltpu.SemaphoreType.DMA((4,)),
             pltpu.SemaphoreType.DMA((1,)),
             pltpu.SemaphoreType.DMA((n - 1,)),
             pltpu.SemaphoreType.REGULAR((4,)),

time: 83.1 us -> 83.1 us (level)
  no operation moved by 1% of the time
where the time goes in v7:
time: 83.1 us; the launch traced here: 83 us
  Pallas kernels  83 us (100%)
    pallas_call x1, Pallas kernels, fused(): pl.pallas_call(functools.partial(kernel, n, kv, groups, chunks), out_shap...  80.8 us
    pallas_call x1, Pallas kernels, fused(): pl.pallas_call(finish, out_shape=jax.ShapeDtypeStruct((length, heads), jn...  2.17 us

profile of v7, /device:TPU:1, one launch (start us, length us, event | category | flops | bytes accessed | tf_op | source)
XLA Modules:
  0.0 83.0 jit_solution(17181755697070792148)
XLA Ops:
  0.0 80.8 %shard_map.64 = (bf16[1024,1024]{1,0:T(8,128)(2,1)S(1)}, bf16[4,256,128]{2,1,0:T(8,128)(2,1)S(1)}, bf16[4,1024,128]{2,1,0:T(8,128)(2,1)S(1)}, bf16[4,1024,256]{2,1,0:T(8,128)(2,1)S(1)}) custom-call(bf16[576,1024]{1,0:T(8,128)(2,1)} %bitcast.1, f32[2304]{0:T(1024)} %gain_in.1, f32[2,1024,128]{2,1,0:T(8,128)} %constant.2.clone.trig_in, ...), custom_call_target="tpu_custom_call" | custom-call | flops 9663676416 | bytes 1179648 | tf_op jit(solution)/shard_map/pallas_call | solution.py:570
  80.8 2.2 %shard_map.65 = bf16[1024,1024]{1,0:T(8,128)(2,1)} custom-call(bf16[1024,1024]{1,0:T(8,128)(2,1)S(1)} %get-tuple-element.9.out_ref, bf16[4,256,128]{2,1,0:T(8,128)(2,1)S(1)} %get-tuple-element.10.q_s, bf16[4,1024,128]{2,1,0:T(8,128)(2,1)S(1)} %get-tuple-element.11.k_s, bf16[4,1024,256]{2,1,0:T(8,128)(2,1)S(1)} %get-tuple-element.12.v_s), custom_call_target="tpu_custom_call" | custom-call | tf_op jit(solution)/shard_map/pallas_call | solution.py:604
